TPU v7x, 768 devices: a whole 4x8x12 slice. The times are simulated.
768 devices in a mesh: section: 96 (over y_hi, z, core), mp: 8 (over y_lo, x).
Axes of the slice: x: 4, y: 8 (y_hi: 4, y_lo: 2; y = y_hi * 2 + y_lo), z: 12, core: 2. Of those that a mesh axis runs over, the one named last changes fastest.
Arguments:
- arrive_rows: bfloat16 [96, 64, 1024], P('section'), may hold values from -50 to 50
- arrive_grads: bfloat16 [96, 64, 1024], P('section'), may hold values from -6 to 6
- feed_rows: bfloat16 [4, 64, 1024], replicated, may hold values from -50 to 50
- feed_grads: bfloat16 [4, 64, 1024], replicated, may hold values from -6 to 6
- stashed_rows: bfloat16 [96, 5, 64, 1024], P('section'), may hold values from -50 to 50
- slot_order: int32 [96, 5], P('section'), may hold values from 0 to 4, each once within a row
- enter_weight: bfloat16 [96, 1024, 4096], P('section', None, 'mp'), may hold values from -0.1875 to 0.1875
- leave_weight: bfloat16 [96, 4096, 1024], P('section', 'mp'), may hold values from -0.09375 to 0.09375
- norm_gain: bfloat16 [96, 1024], P('section'), may hold values from 0.099609375 to 1.8984375
Outputs:
- depart_rows: bfloat16 [96, 64, 1024], P('section')
- depart_grads: bfloat16 [96, 64, 1024], P('section')
- enter_update: bfloat16 [96, 1024, 4096], P('section', None, 'mp')
- leave_update: bfloat16 [96, 4096, 1024], P('section', 'mp')
- gain_update: float32 [96, 1024], P('section')
Inputs may be any that keep to these rules, and one draw needn't show every extreme that they name: `slot_order`: each section's row is a permutation of 0 to 4.
All inputs are finite; a program needn't handle non-finite values.
Results may differ from a plain program's by a relative error of at most 0.025.
Values may be sent and summed in bfloat16 or wider, within the bound.
No kernel may reach another device: no remote copies, remote signals or barrier semaphores. Data moves between devices by JAX's collectives and lax.ppermute only.
A program may use at most 64 MiB of HBM per device.

v0:
```python
import math

import jax
import jax.numpy as jnp
from jax import lax
from jax.sharding import PartitionSpec as P

D = 1024


epsilon = 1e-06


def split_up(value, dim, peers):
    lengths = value.shape
    parts = value.reshape(*lengths[:dim], peers, lengths[dim] // peers, *lengths[dim + 1 :])
    return jnp.moveaxis(parts, dim, 0)


def sum_at_owner(value, axis, dim):
    peers = lax.axis_size(axis)
    parts = lax.all_to_all(split_up(value, dim, peers), axis, 0, 0, tiled=True)
    return jnp.sum(parts.astype(jnp.float32), axis=0)


def joined_along(parts, dim):
    parts = jnp.moveaxis(parts, 0, dim)
    lengths = parts.shape
    return parts.reshape(*lengths[:dim], lengths[dim] * lengths[dim + 1], *lengths[dim + 2 :])


def from_everyone(value, axis):
    peers = lax.axis_size(axis)
    return lax.all_to_all(
        jnp.broadcast_to(value[None], (peers, *value.shape)), axis, 0, 0, tiled=True
    )


def gathered_copies(value, axis, dim):
    return joined_along(from_everyone(value, axis), dim)


def sent_together(arrays, axis, dim, along):
    widths = [math.prod(a.shape[along:]) for a in arrays]
    both = jnp.concatenate(
        [a.reshape(*a.shape[:along], w) for a, w in zip(arrays, widths)], axis=along
    )
    filled = sum_at_owner(both, axis, dim)
    parts = jnp.split(filled, [sum(widths[:k]) for k in range(1, len(widths))], axis=along)
    return tuple(
        (b.reshape(*filled.shape[:along], *a.shape[along:]) for a, b in zip(arrays, parts))
    )


def shifted(block, axis, distance):
    devices = range(lax.axis_size(axis))
    route = [(i - distance, i) for i in devices if i - distance in devices]
    return lax.ppermute(block, axis, route)


def taken_together(value, axis):
    return from_everyone(value, axis).sum(axis=0)


def against_rows(left, right):
    return lax.dot_general(
        left, right, (((1,), (1,)), ((), ())), preferred_element_type=jnp.float32
    )


def across_rows(left, right):
    return lax.dot_general(
        left, right, (((0,), (0,)), ((), ())), preferred_element_type=jnp.float32
    )


def pick_slot(values, slot_index):
    return lax.dynamic_index_in_dim(values, slot_index, 0, keepdims=False)


def local(
    arrive_rows,
    arrive_grads,
    feed_rows,
    feed_grads,
    stashed_rows,
    slot_order,
    enter_weight,
    leave_weight,
    norm_gain,
):
    section_count = lax.axis_size("section")
    position = lax.axis_index("section")
    first_section = position == 0
    last_section = position == section_count - 1
    weight_in = enter_weight[0]
    weight_out = leave_weight[0]
    gain_row = norm_gain[0].astype(jnp.float32)
    stashed = stashed_rows[0]
    plan = slot_order[0]
    step_count = stashed.shape[0]
    row_count = stashed.shape[1]
    groups = lax.axis_size("mp")
    share = row_count // groups
    row_start = lax.axis_index("mp") * share

    def normalize(rows_in):
        wide = rows_in.astype(jnp.float32)
        scaled = (wide * gain_row).astype(jnp.bfloat16)
        inverse = lax.rsqrt(jnp.sum(wide * wide, axis=1) / D + epsilon)
        projected = jnp.dot(scaled, weight_in, preferred_element_type=jnp.float32)
        return (wide, scaled, inverse, projected)

    def own_rows(values):
        return lax.dynamic_slice_in_dim(values, row_start, share, 0)

    inputs_now = arrive_rows[0]
    grads_now = arrive_grads[0]
    gain_total = jnp.zeros_like(gain_row)
    enter_total = jnp.zeros(weight_in.shape, jnp.float32)
    leave_total = jnp.zeros(weight_out.shape, jnp.float32)
    outputs = inputs_now
    input_grad = grads_now
    for step in range(step_count):
        wide, scaled, inverse, projected = normalize(inputs_now)
        fresh_hidden = jax.nn.gelu(inverse[:, None] * projected).astype(jnp.bfloat16)
        branch_local = jnp.dot(fresh_hidden, weight_out, preferred_element_type=jnp.float32)
        branch_share = sum_at_owner(branch_local.astype(jnp.bfloat16), "mp", 0)
        out_share = (own_rows(wide) + branch_share).astype(jnp.bfloat16)
        outputs = gathered_copies(out_share, "mp", 0)
        slot_index = plan[step]
        slot_rows = pick_slot(stashed, slot_index)
        slot_wide, slot_scaled, slot_inverse, slot_proj = normalize(slot_rows)
        slot_preact = slot_inverse[:, None] * slot_proj
        hidden_wide, slope_fn = jax.vjp(jax.nn.gelu, slot_preact)
        slot_hidden = hidden_wide.astype(jnp.bfloat16)
        hidden_grad = against_rows(grads_now, weight_out)
        pre_grad = slope_fn(hidden_grad)[0]
        scaled_grad = (slot_inverse[:, None] * pre_grad).astype(jnp.bfloat16)
        inverse_local = jnp.sum(pre_grad * slot_proj, axis=1)
        input_local = against_rows(scaled_grad, weight_in)
        part_share, inverse_share = sent_together(
            (input_local.astype(jnp.bfloat16), inverse_local.astype(jnp.bfloat16)), "mp", 0, 1
        )
        own_inverse = own_rows(slot_inverse)
        own_wide = own_rows(slot_wide)
        factor_share = -inverse_share * own_inverse * own_inverse * own_inverse / D
        grad_share = (
            own_rows(grads_now).astype(jnp.float32)
            + part_share * gain_row
            + factor_share[:, None] * own_wide
        ).astype(jnp.bfloat16)
        gain_total = gain_total + jnp.sum(part_share * own_wide, axis=0)
        input_grad = gathered_copies(grad_share, "mp", 0)
        leave_total = leave_total + across_rows(slot_hidden, grads_now)
        enter_total = enter_total + across_rows(slot_scaled, scaled_grad)
        if step + 1 < step_count:
            moved_rows = shifted(outputs, "section", 1)
            inputs_now = jnp.where(first_section, feed_rows[step], moved_rows)
            returned = shifted(input_grad, "section", -1)
            grads_now = jnp.where(last_section, feed_grads[step], returned)
    gain_total = taken_together(gain_total, "mp")
    return (
        outputs[None],
        input_grad[None],
        enter_total.astype(jnp.bfloat16)[None],
        leave_total.astype(jnp.bfloat16)[None],
        gain_total[None],
    )


def solution(mesh):
    placed = (
        P("section", None, None),
        P("section", None, None),
        P(),
        P(),
        P("section", None, None, None),
        P("section", None),
        P("section", None, "mp"),
        P("section", "mp", None),
        P("section", None),
    )
    return jax.shard_map(
        local,
        mesh=mesh,
        in_specs=placed,
        out_specs=(
            P("section", None, None),
            P("section", None, None),
            P("section", None, "mp"),
            P("section", "mp", None),
            P("section", None),
        ),
        check_vma=False,
    )
```

profile of v0, /device:TPU:42, one launch (start us, length us, event | category | flops | bytes accessed | tf_op | source)
XLA Modules:
  0.0 290.6 jit_solution(4022897837392880610)
XLA Ops:
  5.1 5.7 %all-to-all-start = ((bf16[8,8,1024]{2,1,0:T(8,128)(2,1)}), bf16[8,8,1024]{2,1,0:T(8,128)(2,1)S(1)}, u32[]{:S(2)}, u32[]{:S(2)}) async-start(bf16[8,8,1024]{2,1,0:T(8,128)(2,1)} %fusion.1), calls=%async_computation | async-start | bytes 262144 | tf_op jit(solution)/shard_map/all_to_all | solution.py:22
  31.8 5.7 %all-to-all-start.10 = ((bf16[8,8,1025]{2,1,0:T(8,128)(2,1)}), bf16[8,8,1025]{2,1,0:T(8,128)(2,1)S(1)}, u32[]{:S(2)}, u32[]{:S(2)}) async-start(bf16[8,8,1025]{2,1,0:T(8,128)(2,1)} %pad_maximum_fusion), calls=%async_computation.10 | async-start | bytes 294912 | tf_op jit(solution)/shard_map/all_to_all | solution.py:22
  42.8 5.4 %all-to-all-start.1 = ((bf16[8,8,1024]{2,1,0:T(8,128)(2,1)}), bf16[8,8,1024]{2,1,0:T(8,128)(2,1)S(1)}, u32[]{:S(2)}, u32[]{:S(2)}) async-start(bf16[8,8,1024]{2,1,0:T(8,128)(2,1)} %broadcast_in_dim.28), calls=%async_computation.1 | async-start | bytes 262144 | tf_op jit(solution)/shard_map/all_to_all | solution.py:34
  53.3 6.0 %all-to-all-start.11 = ((bf16[8,8,1024]{2,1,0:T(8,128)(2,1)}), bf16[8,8,1024]{2,1,0:T(8,128)(2,1)}, u32[]{:S(2)}, u32[]{:S(2)}) async-start(bf16[8,8,1024]{2,1,0:T(8,128)(2,1)} %broadcast_in_dim.33), calls=%async_computation.11 | async-start | bytes 262144 | tf_op jit(solution)/shard_map/all_to_all | solution.py:34
  63.9 10.4 %collective-permute-start.4 = (bf16[64,1024]{1,0:T(8,128)(2,1)}, bf16[64,1024]{1,0:T(8,128)(2,1)}, u32[]{:S(2)}, u32[]{:S(2)}) collective-permute-start(bf16[64,1024]{1,0:T(8,128)(2,1)} %bitcast.30), channel_id=1, source_target_pairs={{8,0},{16,8},{24,16},{32,24},{40,32},{48,40},{56,48},{64,56},{72,6... | collective-permute-start | bytes 393224 | tf_op jit(solution)/shard_map/ppermute | solution.py:58
  76.7 6.0 %all-to-all-start.2 = ((bf16[8,8,1024]{2,1,0:T(8,128)(2,1)}), bf16[8,8,1024]{2,1,0:T(8,128)(2,1)}, u32[]{:S(2)}, u32[]{:S(2)}) async-start(bf16[8,8,1024]{2,1,0:T(8,128)(2,1)} %fusion.2), calls=%async_computation.2 | async-start | bytes 262144 | tf_op jit(solution)/shard_map/all_to_all | solution.py:22
  87.5 5.7 %all-to-all-start.12 = ((bf16[8,8,1025]{2,1,0:T(8,128)(2,1)}), bf16[8,8,1025]{2,1,0:T(8,128)(2,1)S(1)}, u32[]{:S(2)}, u32[]{:S(2)}) async-start(bf16[8,8,1025]{2,1,0:T(8,128)(2,1)} %pad_maximum_fusion.1), calls=%async_computation.12 | async-start | bytes 294912 | tf_op jit(solution)/shard_map/all_to_all | solution.py:22
  99.1 5.3 %all-to-all-start.3 = ((bf16[8,8,1024]{2,1,0:T(8,128)(2,1)}), bf16[8,8,1024]{2,1,0:T(8,128)(2,1)S(1)}, u32[]{:S(2)}, u32[]{:S(2)}) async-start(bf16[8,8,1024]{2,1,0:T(8,128)(2,1)} %broadcast_in_dim.29), calls=%async_computation.3 | async-start | bytes 262144 | tf_op jit(solution)/shard_map/all_to_all | solution.py:34
  109.6 5.4 %all-to-all-start.13 = ((bf16[8,8,1024]{2,1,0:T(8,128)(2,1)}), bf16[8,8,1024]{2,1,0:T(8,128)(2,1)S(1)}, u32[]{:S(2)}, u32[]{:S(2)}) async-start(bf16[8,8,1024]{2,1,0:T(8,128)(2,1)} %broadcast_in_dim.34), calls=%async_computation.13 | async-start | bytes 262144 | tf_op jit(solution)/shard_map/all_to_all | solution.py:34
  119.6 8.0 %collective-permute-start.5 = (bf16[64,1024]{1,0:T(8,128)(2,1)S(1)}, bf16[64,1024]{1,0:T(8,128)(2,1)}, u32[]{:S(2)}, u32[]{:S(2)}) collective-permute-start(bf16[64,1024]{1,0:T(8,128)(2,1)S(1)} %bitcast.323), channel_id=1, source_target_pairs={{8,0},{16,8},{24,16},{32,24},{40,32},{48,40},{56,48},{64,56},{72,6... | collective-permute-start | bytes 393224 | tf_op jit(solution)/shard_map/ppermute | solution.py:58
  130.0 5.7 %all-to-all-start.4 = ((bf16[8,8,1024]{2,1,0:T(8,128)(2,1)}), bf16[8,8,1024]{2,1,0:T(8,128)(2,1)}, u32[]{:S(2)}, u32[]{:S(2)}) async-start(bf16[8,8,1024]{2,1,0:T(8,128)(2,1)} %fusion.3), calls=%async_computation.4 | async-start | bytes 262144 | tf_op jit(solution)/shard_map/all_to_all | solution.py:22
  140.4 5.7 %all-to-all-start.14 = ((bf16[8,8,1025]{2,1,0:T(8,128)(2,1)}), bf16[8,8,1025]{2,1,0:T(8,128)(2,1)S(1)}, u32[]{:S(2)}, u32[]{:S(2)}) async-start(bf16[8,8,1025]{2,1,0:T(8,128)(2,1)} %pad_maximum_fusion.2), calls=%async_computation.14 | async-start | bytes 294912 | tf_op jit(solution)/shard_map/all_to_all | solution.py:22
  151.4 5.4 %all-to-all-start.5 = ((bf16[8,8,1024]{2,1,0:T(8,128)(2,1)}), bf16[8,8,1024]{2,1,0:T(8,128)(2,1)S(1)}, u32[]{:S(2)}, u32[]{:S(2)}) async-start(bf16[8,8,1024]{2,1,0:T(8,128)(2,1)} %broadcast_in_dim.30), calls=%async_computation.5 | async-start | bytes 262144 | tf_op jit(solution)/shard_map/all_to_all | solution.py:34
  162.0 5.4 %all-to-all-start.15 = ((bf16[8,8,1024]{2,1,0:T(8,128)(2,1)}), bf16[8,8,1024]{2,1,0:T(8,128)(2,1)S(1)}, u32[]{:S(2)}, u32[]{:S(2)}) async-start(bf16[8,8,1024]{2,1,0:T(8,128)(2,1)} %broadcast_in_dim.35), calls=%async_computation.15 | async-start | bytes 262144 | tf_op jit(solution)/shard_map/all_to_all | solution.py:34
  172.1 8.0 %collective-permute-start.6 = (bf16[64,1024]{1,0:T(8,128)(2,1)S(1)}, bf16[64,1024]{1,0:T(8,128)(2,1)}, u32[]{:S(2)}, u32[]{:S(2)}) collective-permute-start(bf16[64,1024]{1,0:T(8,128)(2,1)S(1)} %bitcast.324), channel_id=1, source_target_pairs={{8,0},{16,8},{24,16},{32,24},{40,32},{48,40},{56,48},{64,56},{72,6... | collective-permute-start | bytes 393224 | tf_op jit(solution)/shard_map/ppermute | solution.py:58
  182.5 5.7 %all-to-all-start.6 = ((bf16[8,8,1024]{2,1,0:T(8,128)(2,1)}), bf16[8,8,1024]{2,1,0:T(8,128)(2,1)}, u32[]{:S(2)}, u32[]{:S(2)}) async-start(bf16[8,8,1024]{2,1,0:T(8,128)(2,1)} %fusion.4), calls=%async_computation.6 | async-start | bytes 262144 | tf_op jit(solution)/shard_map/all_to_all | solution.py:22
  192.8 5.4 %all-to-all-start.16 = ((bf16[8,8,1025]{2,1,0:T(8,128)(2,1)}), bf16[8,8,1025]{2,1,0:T(8,128)(2,1)S(1)}, u32[]{:S(2)}, u32[]{:S(2)}) async-start(bf16[8,8,1025]{2,1,0:T(8,128)(2,1)} %pad_maximum_fusion.3), calls=%async_computation.16 | async-start | bytes 294912 | tf_op jit(solution)/shard_map/all_to_all | solution.py:22
  203.5 5.4 %all-to-all-start.7 = ((bf16[8,8,1024]{2,1,0:T(8,128)(2,1)}), bf16[8,8,1024]{2,1,0:T(8,128)(2,1)S(1)}, u32[]{:S(2)}, u32[]{:S(2)}) async-start(bf16[8,8,1024]{2,1,0:T(8,128)(2,1)} %broadcast_in_dim.31), calls=%async_computation.7 | async-start | bytes 262144 | tf_op jit(solution)/shard_map/all_to_all | solution.py:34
  224.3 7.8 %collective-permute-start.7 = (bf16[64,1024]{1,0:T(8,128)(2,1)S(1)}, bf16[64,1024]{1,0:T(8,128)(2,1)}, u32[]{:S(2)}, u32[]{:S(2)}) collective-permute-start(bf16[64,1024]{1,0:T(8,128)(2,1)S(1)} %bitcast.325), channel_id=1, source_target_pairs={{8,0},{16,8},{24,16},{32,24},{40,32},{48,40},{56,48},{64,56},{72,6... | collective-permute-start | bytes 393224 | tf_op jit(solution)/shard_map/ppermute | solution.py:58
  234.6 5.7 %all-to-all-start.8 = ((bf16[8,8,1024]{2,1,0:T(8,128)(2,1)}), bf16[8,8,1024]{2,1,0:T(8,128)(2,1)}, u32[]{:S(2)}, u32[]{:S(2)}) async-start(bf16[8,8,1024]{2,1,0:T(8,128)(2,1)} %fusion.5), calls=%async_computation.8 | async-start | bytes 262144 | tf_op jit(solution)/shard_map/all_to_all | solution.py:22
  244.9 5.4 %all-to-all-start.18 = ((bf16[8,8,1025]{2,1,0:T(8,128)(2,1)}), bf16[8,8,1025]{2,1,0:T(8,128)(2,1)S(1)}, u32[]{:S(2)}, u32[]{:S(2)}) async-start(bf16[8,8,1025]{2,1,0:T(8,128)(2,1)} %pad_maximum_fusion.4), calls=%async_computation.18 | async-start | bytes 294912 | tf_op jit(solution)/shard_map/all_to_all | solution.py:22
  256.6 5.4 %all-to-all-start.20 = ((f32[8,1,1024]{2,1,0:T(1,128)}), f32[8,1,1024]{2,1,0:T(1,128)S(1)}, u32[]{:S(2)}, u32[]{:S(2)}) async-start(f32[8,1,1024]{2,1,0:T(1,128)} %broadcast_in_dim.40), calls=%async_computation.20 | async-start | bytes 65536 | tf_op jit(solution)/shard_map/all_to_all | solution.py:34
  266.6 5.6 %all-to-all-start.9 = ((bf16[8,8,1024]{2,1,0:T(8,128)(2,1)}), bf16[8,8,1024]{2,1,0:T(8,128)(2,1)S(1)}, u32[]{:S(2)}, u32[]{:S(2)}) async-start(bf16[8,8,1024]{2,1,0:T(8,128)(2,1)} %broadcast_in_dim.32), calls=%async_computation.9 | async-start | bytes 262144 | tf_op jit(solution)/shard_map/all_to_all | solution.py:34
  278.0 5.7 %all-to-all-start.19 = ((bf16[8,8,1024]{2,1,0:T(8,128)(2,1)}), bf16[8,8,1024]{2,1,0:T(8,128)(2,1)S(1)}, u32[]{:S(2)}, u32[]{:S(2)}) async-start(bf16[8,8,1024]{2,1,0:T(8,128)(2,1)} %broadcast_in_dim.37), calls=%async_computation.19 | async-start | bytes 262144 | tf_op jit(solution)/shard_map/all_to_all | solution.py:34
  (165 shorter events, 133.8 us)
Async XLA Ops:
  5.1 26.7 %all-to-all-start = ((bf16[8,8,1024]{2,1,0:T(8,128)(2,1)}), bf16[8,8,1024]{2,1,0:T(8,128)(2,1)S(1)}, u32[]{:S(2)}, u32[]{:S(2)}) async-start(bf16[8,8,1024]{2,1,0:T(8,128)(2,1)} %fusion.1), calls=%async_computation | async-start | bytes 262144 | tf_op jit(solution)/shard_map/all_to_all | solution.py:22
  31.8 10.3 %all-to-all-start.10 = ((bf16[8,8,1025]{2,1,0:T(8,128)(2,1)}), bf16[8,8,1025]{2,1,0:T(8,128)(2,1)S(1)}, u32[]{:S(2)}, u32[]{:S(2)}) async-start(bf16[8,8,1025]{2,1,0:T(8,128)(2,1)} %pad_maximum_fusion), calls=%async_computation.10 | async-start | bytes 294912 | tf_op jit(solution)/shard_map/all_to_all | solution.py:22
  53.3 10.6 %all-to-all-start.11 = ((bf16[8,8,1024]{2,1,0:T(8,128)(2,1)}), bf16[8,8,1024]{2,1,0:T(8,128)(2,1)}, u32[]{:S(2)}, u32[]{:S(2)}) async-start(bf16[8,8,1024]{2,1,0:T(8,128)(2,1)} %broadcast_in_dim.33), calls=%async_computation.11 | async-start | bytes 262144 | tf_op jit(solution)/shard_map/all_to_all | solution.py:34
  59.3 15.1 %collective-permute-start = (bf16[64,1024]{1,0:T(8,128)(2,1)S(1)}, bf16[64,1024]{1,0:T(8,128)(2,1)}, u32[]{:S(2)}, u32[]{:S(2)}) collective-permute-start(bf16[64,1024]{1,0:T(8,128)(2,1)S(1)} %bitcast.319), channel_id=1, source_target_pairs={{0,8},{8,16},{16,24},{24,32},{32,40},{40,48},{48,56},{56,64},{64,7... | collective-permute-start | bytes 393224 | tf_op jit(solution)/shard_map/ppermute | solution.py:58
  63.9 18.8 %collective-permute-start.4 = (bf16[64,1024]{1,0:T(8,128)(2,1)}, bf16[64,1024]{1,0:T(8,128)(2,1)}, u32[]{:S(2)}, u32[]{:S(2)}) collective-permute-start(bf16[64,1024]{1,0:T(8,128)(2,1)} %bitcast.30), channel_id=1, source_target_pairs={{8,0},{16,8},{24,16},{32,24},{40,32},{48,40},{56,48},{64,56},{72,6... | collective-permute-start | bytes 393224 | tf_op jit(solution)/shard_map/ppermute | solution.py:58
  76.7 10.7 %all-to-all-start.2 = ((bf16[8,8,1024]{2,1,0:T(8,128)(2,1)}), bf16[8,8,1024]{2,1,0:T(8,128)(2,1)}, u32[]{:S(2)}, u32[]{:S(2)}) async-start(bf16[8,8,1024]{2,1,0:T(8,128)(2,1)} %fusion.2), calls=%async_computation.2 | async-start | bytes 262144 | tf_op jit(solution)/shard_map/all_to_all | solution.py:22
  87.5 11.0 %all-to-all-start.12 = ((bf16[8,8,1025]{2,1,0:T(8,128)(2,1)}), bf16[8,8,1025]{2,1,0:T(8,128)(2,1)S(1)}, u32[]{:S(2)}, u32[]{:S(2)}) async-start(bf16[8,8,1025]{2,1,0:T(8,128)(2,1)} %pad_maximum_fusion.1), calls=%async_computation.12 | async-start | bytes 294912 | tf_op jit(solution)/shard_map/all_to_all | solution.py:22
  109.6 10.0 %all-to-all-start.13 = ((bf16[8,8,1024]{2,1,0:T(8,128)(2,1)}), bf16[8,8,1024]{2,1,0:T(8,128)(2,1)S(1)}, u32[]{:S(2)}, u32[]{:S(2)}) async-start(bf16[8,8,1024]{2,1,0:T(8,128)(2,1)} %broadcast_in_dim.34), calls=%async_computation.13 | async-start | bytes 262144 | tf_op jit(solution)/shard_map/all_to_all | solution.py:34
  115.0 12.6 %collective-permute-start.1 = (bf16[64,1024]{1,0:T(8,128)(2,1)S(1)}, bf16[64,1024]{1,0:T(8,128)(2,1)}, u32[]{:S(2)}, u32[]{:S(2)}) collective-permute-start(bf16[64,1024]{1,0:T(8,128)(2,1)S(1)} %bitcast.320), channel_id=1, source_target_pairs={{0,8},{8,16},{16,24},{24,32},{32,40},{40,48},{48,56},{56,64},{64,7... | collective-permute-start | bytes 393224 | tf_op jit(solution)/shard_map/ppermute | solution.py:58
  119.6 16.1 %collective-permute-start.5 = (bf16[64,1024]{1,0:T(8,128)(2,1)S(1)}, bf16[64,1024]{1,0:T(8,128)(2,1)}, u32[]{:S(2)}, u32[]{:S(2)}) collective-permute-start(bf16[64,1024]{1,0:T(8,128)(2,1)S(1)} %bitcast.323), channel_id=1, source_target_pairs={{8,0},{16,8},{24,16},{32,24},{40,32},{48,40},{56,48},{64,56},{72,6... | collective-permute-start | bytes 393224 | tf_op jit(solution)/shard_map/ppermute | solution.py:58
  130.0 10.4 %all-to-all-start.4 = ((bf16[8,8,1024]{2,1,0:T(8,128)(2,1)}), bf16[8,8,1024]{2,1,0:T(8,128)(2,1)}, u32[]{:S(2)}, u32[]{:S(2)}) async-start(bf16[8,8,1024]{2,1,0:T(8,128)(2,1)} %fusion.3), calls=%async_computation.4 | async-start | bytes 262144 | tf_op jit(solution)/shard_map/all_to_all | solution.py:22
  140.4 10.3 %all-to-all-start.14 = ((bf16[8,8,1025]{2,1,0:T(8,128)(2,1)}), bf16[8,8,1025]{2,1,0:T(8,128)(2,1)S(1)}, u32[]{:S(2)}, u32[]{:S(2)}) async-start(bf16[8,8,1025]{2,1,0:T(8,128)(2,1)} %pad_maximum_fusion.2), calls=%async_computation.14 | async-start | bytes 294912 | tf_op jit(solution)/shard_map/all_to_all | solution.py:22
  162.0 10.1 %all-to-all-start.15 = ((bf16[8,8,1024]{2,1,0:T(8,128)(2,1)}), bf16[8,8,1024]{2,1,0:T(8,128)(2,1)S(1)}, u32[]{:S(2)}, u32[]{:S(2)}) async-start(bf16[8,8,1024]{2,1,0:T(8,128)(2,1)} %broadcast_in_dim.35), calls=%async_computation.15 | async-start | bytes 262144 | tf_op jit(solution)/shard_map/all_to_all | solution.py:34
  167.4 12.7 %collective-permute-start.2 = (bf16[64,1024]{1,0:T(8,128)(2,1)S(1)}, bf16[64,1024]{1,0:T(8,128)(2,1)}, u32[]{:S(2)}, u32[]{:S(2)}) collective-permute-start(bf16[64,1024]{1,0:T(8,128)(2,1)S(1)} %bitcast.321), channel_id=1, source_target_pairs={{0,8},{8,16},{16,24},{24,32},{32,40},{40,48},{48,56},{56,64},{64,7... | collective-permute-start | bytes 393224 | tf_op jit(solution)/shard_map/ppermute | solution.py:58
  172.1 16.1 %collective-permute-start.6 = (bf16[64,1024]{1,0:T(8,128)(2,1)S(1)}, bf16[64,1024]{1,0:T(8,128)(2,1)}, u32[]{:S(2)}, u32[]{:S(2)}) collective-permute-start(bf16[64,1024]{1,0:T(8,128)(2,1)S(1)} %bitcast.324), channel_id=1, source_target_pairs={{8,0},{16,8},{24,16},{32,24},{40,32},{48,40},{56,48},{64,56},{72,6... | collective-permute-start | bytes 393224 | tf_op jit(solution)/shard_map/ppermute | solution.py:58
  182.5 10.3 %all-to-all-start.6 = ((bf16[8,8,1024]{2,1,0:T(8,128)(2,1)}), bf16[8,8,1024]{2,1,0:T(8,128)(2,1)}, u32[]{:S(2)}, u32[]{:S(2)}) async-start(bf16[8,8,1024]{2,1,0:T(8,128)(2,1)} %fusion.4), calls=%async_computation.6 | async-start | bytes 262144 | tf_op jit(solution)/shard_map/all_to_all | solution.py:22
  192.8 10.0 %all-to-all-start.16 = ((bf16[8,8,1025]{2,1,0:T(8,128)(2,1)}), bf16[8,8,1025]{2,1,0:T(8,128)(2,1)S(1)}, u32[]{:S(2)}, u32[]{:S(2)}) async-start(bf16[8,8,1025]{2,1,0:T(8,128)(2,1)} %pad_maximum_fusion.3), calls=%async_computation.16 | async-start | bytes 294912 | tf_op jit(solution)/shard_map/all_to_all | solution.py:22
  203.5 10.3 %all-to-all-start.7 = ((bf16[8,8,1024]{2,1,0:T(8,128)(2,1)}), bf16[8,8,1024]{2,1,0:T(8,128)(2,1)S(1)}, u32[]{:S(2)}, u32[]{:S(2)}) async-start(bf16[8,8,1024]{2,1,0:T(8,128)(2,1)} %broadcast_in_dim.31), calls=%async_computation.7 | async-start | bytes 262144 | tf_op jit(solution)/shard_map/all_to_all | solution.py:34
  219.4 12.8 %collective-permute-start.3 = (bf16[64,1024]{1,0:T(8,128)(2,1)S(1)}, bf16[64,1024]{1,0:T(8,128)(2,1)}, u32[]{:S(2)}, u32[]{:S(2)}) collective-permute-start(bf16[64,1024]{1,0:T(8,128)(2,1)S(1)} %bitcast.322), channel_id=1, source_target_pairs={{0,8},{8,16},{16,24},{24,32},{32,40},{40,48},{48,56},{56,64},{64,7... | collective-permute-start | bytes 393224 | tf_op jit(solution)/shard_map/ppermute | solution.py:58
  224.3 16.0 %collective-permute-start.7 = (bf16[64,1024]{1,0:T(8,128)(2,1)S(1)}, bf16[64,1024]{1,0:T(8,128)(2,1)}, u32[]{:S(2)}, u32[]{:S(2)}) collective-permute-start(bf16[64,1024]{1,0:T(8,128)(2,1)S(1)} %bitcast.325), channel_id=1, source_target_pairs={{8,0},{16,8},{24,16},{32,24},{40,32},{48,40},{56,48},{64,56},{72,6... | collective-permute-start | bytes 393224 | tf_op jit(solution)/shard_map/ppermute | solution.py:58
  234.6 10.3 %all-to-all-start.8 = ((bf16[8,8,1024]{2,1,0:T(8,128)(2,1)}), bf16[8,8,1024]{2,1,0:T(8,128)(2,1)}, u32[]{:S(2)}, u32[]{:S(2)}) async-start(bf16[8,8,1024]{2,1,0:T(8,128)(2,1)} %fusion.5), calls=%async_computation.8 | async-start | bytes 262144 | tf_op jit(solution)/shard_map/all_to_all | solution.py:22
  244.9 10.0 %all-to-all-start.18 = ((bf16[8,8,1025]{2,1,0:T(8,128)(2,1)}), bf16[8,8,1025]{2,1,0:T(8,128)(2,1)S(1)}, u32[]{:S(2)}, u32[]{:S(2)}) async-start(bf16[8,8,1025]{2,1,0:T(8,128)(2,1)} %pad_maximum_fusion.4), calls=%async_computation.18 | async-start | bytes 294912 | tf_op jit(solution)/shard_map/all_to_all | solution.py:22
  266.6 10.7 %all-to-all-start.9 = ((bf16[8,8,1024]{2,1,0:T(8,128)(2,1)}), bf16[8,8,1024]{2,1,0:T(8,128)(2,1)S(1)}, u32[]{:S(2)}, u32[]{:S(2)}) async-start(bf16[8,8,1024]{2,1,0:T(8,128)(2,1)} %broadcast_in_dim.32), calls=%async_computation.9 | async-start | bytes 262144 | tf_op jit(solution)/shard_map/all_to_all | solution.py:34
  278.0 11.3 %all-to-all-start.19 = ((bf16[8,8,1024]{2,1,0:T(8,128)(2,1)}), bf16[8,8,1024]{2,1,0:T(8,128)(2,1)S(1)}, u32[]{:S(2)}, u32[]{:S(2)}) async-start(bf16[8,8,1024]{2,1,0:T(8,128)(2,1)} %broadcast_in_dim.37), calls=%async_computation.19 | async-start | bytes 262144 | tf_op jit(solution)/shard_map/all_to_all | solution.py:34
  (16 other events, 126.9 us)
where the time goes:
time: 294 us; the launch traced here: 291 us
  starting transfers between devices  159 us (54%)
  matrix products  44 us (15%)
  waiting for transfers between devices  40.1 us (14%)
  other arithmetic  26.2 us (9%)
  between operations  10.9 us (4%)
  local copies, waits for them, and re-layouts  10.7 us (4%)
    all_to_all x11, starting transfers between devices, from_everyone(): lax.all_to_all(jnp.broadcast_to(value[None], (peers, *value.shape)), axis...  59.9 us
    all_to_all x10, starting transfers between devices, sum_at_owner(): parts = lax.all_to_all(split_up(value, dim, peers), axis, 0, 0, tiled=True)  56.7 us
    ppermute x8, starting transfers between devices, shifted(): return lax.ppermute(block, axis, route)  42 us
    dot_general x10, matrix products, across_rows(): lax.dot_general(left, right, (((0,), (0,)), ((), ())), preferred_element_...  28.5 us
    all_to_all x11, waiting for transfers between devices, from_everyone(): lax.all_to_all(jnp.broadcast_to(value[None], (peers, *value.shape)), axis...  20.8 us
    all_to_all x10, waiting for transfers between devices, sum_at_owner(): parts = lax.all_to_all(split_up(value, dim, peers), axis, 0, 0, tiled=True)  19.2 us
    dot_general x5, matrix products, local(): jnp.dot(fresh_hidden, weight_out, preferred_element_type=jnp.float32)  7.57 us
    broadcast_in_dim x11, local copies, waits for them, and re-layouts, from_everyone(): jnp.broadcast_to(value[None], (peers, *value.shape))  7.28 us
  transfers between devices with their start and end apart: 29, of which 14 were waited for; matrix products, arithmetic and copies ran while one was open for 23% of the time, Pallas kernels for 0%

commit v1 on v0

v1 whole, which is shorter than its diff:
```python
import jax
import jax.numpy as jnp
from jax import lax
from jax.sharding import PartitionSpec as P

D = 1024
EPSILON = 1e-06
BOTH = ("section", "mp")


def pair_groups(sections, peers, first):
    groups = []
    for k in range(first, sections + first, 2):
        pair = (k % sections, (k + 1) % sections)
        groups.append([s * peers + m for s in pair for m in range(peers)])
    return groups


def against_rows(left, right):
    return lax.dot_general(
        left, right, (((1,), (1,)), ((), ())), preferred_element_type=jnp.float32
    )


def across_rows(left, right):
    return lax.dot_general(
        left, right, (((0,), (0,)), ((), ())), preferred_element_type=jnp.float32
    )


def local(
    arrive_rows,
    arrive_grads,
    feed_rows,
    feed_grads,
    stashed_rows,
    slot_order,
    enter_weight,
    leave_weight,
    norm_gain,
):
    sections = lax.axis_size("section")
    peers = lax.axis_size("mp")
    position = lax.axis_index("section")
    first_section = position == 0
    last_section = position == sections - 1
    even_pairs = pair_groups(sections, peers, 0)
    odd_pairs = pair_groups(sections, peers, 1)
    weight_in = enter_weight[0]
    weight_out = leave_weight[0]
    gain_row = norm_gain[0].astype(jnp.float32)
    stashed = stashed_rows[0]
    steps, rows = stashed.shape[0], stashed.shape[1]
    share = rows // peers
    portion = 1.0 / peers

    def normalize(rows_in):
        wide = rows_in.astype(jnp.float32)
        scaled = (wide * gain_row).astype(jnp.bfloat16)
        inverse = lax.rsqrt(jnp.sum(wide * wide, axis=1) / D + EPSILON)
        projected = jnp.dot(scaled, weight_in, preferred_element_type=jnp.float32)
        return (wide, scaled, inverse, projected)

    def summed(parts):
        return jnp.sum(parts.astype(jnp.float32), axis=0).astype(jnp.bfloat16)

    inputs = arrive_rows[0]
    grads = arrive_grads[0]
    gain_total = jnp.zeros_like(gain_row)
    hidden_list, grad_list, scaled_list, update_list = [], [], [], []
    for step in range(steps):
        wide, _, inverse, projected = normalize(inputs)
        hidden = jax.nn.gelu(inverse[:, None] * projected).astype(jnp.bfloat16)
        forward = jnp.dot(hidden, weight_out, preferred_element_type=jnp.float32)
        forward = (forward + wide * portion).astype(jnp.bfloat16)

        slot = lax.dynamic_index_in_dim(stashed, slot_order[0, step], 0, keepdims=False)
        slot_wide, slot_scaled, slot_inverse, slot_proj = normalize(slot)
        slot_hidden, slope_fn = jax.vjp(jax.nn.gelu, slot_inverse[:, None] * slot_proj)
        hidden_grad = against_rows(grads, weight_out)
        pre_grad = slope_fn(hidden_grad)[0]
        scaled_grad = (slot_inverse[:, None] * pre_grad).astype(jnp.bfloat16)
        factor = -jnp.sum(pre_grad * slot_proj, axis=1) * slot_inverse**3 / D
        input_part = against_rows(scaled_grad, weight_in)
        gain_total = gain_total + jnp.sum(input_part * slot_wide, axis=0)
        backward = (
            grads.astype(jnp.float32) * portion
            + input_part * gain_row
            + factor[:, None] * slot_wide
        ).astype(jnp.bfloat16)
        hidden_list.append(slot_hidden.astype(jnp.bfloat16))
        grad_list.append(grads)
        scaled_list.append(slot_scaled)
        update_list.append(scaled_grad)

        if step + 1 < steps:
            parts = jnp.concatenate([backward, forward], axis=0).reshape(2 * peers, share, D)
            parts = lax.all_to_all(parts, BOTH, 0, 0, axis_index_groups=odd_pairs, tiled=True)
            low, high = summed(parts[:peers]), summed(parts[peers:])
            spread = (peers, share, D)
            parts = jnp.concatenate(
                [jnp.broadcast_to(low[None], spread), jnp.broadcast_to(high[None], spread)], axis=0
            )
            parts = lax.all_to_all(parts, BOTH, 0, 0, axis_index_groups=even_pairs, tiled=True)
            inputs = jnp.where(first_section, feed_rows[step], parts[:peers].reshape(rows, D))
            grads = jnp.where(last_section, feed_grads[step], parts[peers:].reshape(rows, D))

    gain_high = lax.reduce_precision(gain_total, 8, 7)
    gain_low = gain_total - gain_high
    halves = jnp.stack([gain_high, gain_low]).astype(jnp.bfloat16)
    parts = jnp.concatenate(
        [
            forward.reshape(peers, share, D),
            backward.reshape(peers, share, D),
            jnp.broadcast_to(halves[None], (peers, 2, D)),
            jnp.zeros((peers, share - 2, D), jnp.bfloat16),
        ],
        axis=1,
    )
    parts = lax.all_to_all(parts, "mp", 0, 0, tiled=True)
    gain_total = jnp.sum(parts[:, 2 * share : 2 * share + 2].astype(jnp.float32), axis=(0, 1))
    total = summed(parts[:, : 2 * share])
    parts = lax.all_to_all(
        jnp.broadcast_to(total[None], (peers, 2 * share, D)), "mp", 0, 0, tiled=True
    )
    outputs = parts[:, :share].reshape(rows, D)
    input_grad = parts[:, share:].reshape(rows, D)
    leave_total = across_rows(jnp.concatenate(hidden_list), jnp.concatenate(grad_list))
    enter_total = across_rows(jnp.concatenate(scaled_list), jnp.concatenate(update_list))
    return (
        outputs[None],
        input_grad[None],
        enter_total.astype(jnp.bfloat16)[None],
        leave_total.astype(jnp.bfloat16)[None],
        gain_total[None],
    )


def solution(mesh):
    placed = (
        P("section", None, None),
        P("section", None, None),
        P(),
        P(),
        P("section", None, None, None),
        P("section", None),
        P("section", None, "mp"),
        P("section", "mp", None),
        P("section", None),
    )
    return jax.shard_map(
        local,
        mesh=mesh,
        in_specs=placed,
        out_specs=(
            P("section", None, None),
            P("section", None, None),
            P("section", None, "mp"),
            P("section", "mp", None),
            P("section", None),
        ),
        check_vma=False,
    )
```

time: 294 us -> 199 us (0.68)
  the two profiles are of different devices: /device:TPU:42 before, /device:TPU:1 now
where the time goes in v1:
time: 199 us; the launch traced here: 197 us
  starting transfers between devices  56.1 us (28%)
  waiting for transfers between devices  45.6 us (23%)
  matrix products  34.2 us (17%)
  other arithmetic  28.9 us (15%)
  blocking collectives  15.9 us (8%)
  between operations  11.1 us (6%)
  local copies, waits for them, and re-layouts  5.34 us (3%)
    all_to_all x4, starting transfers between devices, local(): lax.all_to_all(parts, BOTH, 0, 0, axis_index_groups=even_pairs, tiled=True)  37.2 us
    all_to_all x4, waiting for transfers between devices, local(): lax.all_to_all(parts, BOTH, 0, 0, axis_index_groups=even_pairs, tiled=True)  22.8 us
    all_to_all x3, waiting for transfers between devices, local(): lax.all_to_all(parts, BOTH, 0, 0, axis_index_groups=odd_pairs, tiled=True)  17.1 us
    all_to_all x1, blocking collectives, local(): lax.all_to_all(parts, BOTH, 0, 0, axis_index_groups=odd_pairs, tiled=True)  15.9 us
    dot_general x10, matrix products, against_rows(): lax.dot_general(left, right, (((1,), (1,)), ((), ())), preferred_element_...  15.7 us
    all_to_all x3, starting transfers between devices, local(): lax.all_to_all(parts, BOTH, 0, 0, axis_index_groups=odd_pairs, tiled=True)  11.4 us
    dot_general x5, matrix products, local(): forward = jnp.dot(hidden, weight_out, preferred_element_type=jnp.float32)  10.1 us
    unnamed x11, other arithmetic  10.1 us
  transfers between devices with their start and end apart: 9, of which 9 were waited for; matrix products, arithmetic and copies ran while one was open for 12% of the time, Pallas kernels for 0%

profile of v1, /device:TPU:1, one launch (start us, length us, event | category | flops | bytes accessed | tf_op | source)
XLA Modules:
  0.0 197.1 jit_solution(12296812752209722942)
XLA Ops:
  20.1 15.9 %all_to_all.50 = bf16[16,8,1024]{2,1,0:T(8,128)(2,1)S(1)} all-to-all(bf16[16,8,1024]{2,1,0:T(8,128)(2,1)S(1)} %maximum_bitcast_fusion), channel_id=1, replica_groups={{8,9,10,11,12,13,14,15,16,17,18,19,20,21,22,23},{24,25,26,27,28,29,30,3..., dimensions={0} | all-to-all | bytes 524288 | tf_op jit(solution)/shard_map/all_to_all | solution.py:98
  36.8 15.7 %all-to-all-start.1 = ((bf16[16,8,1024]{2,1,0:T(8,128)(2,1)}), bf16[16,8,1024]{2,1,0:T(8,128)(2,1)S(1)}, u32[]{:S(2)}, u32[]{:S(2)}) async-start(bf16[16,8,1024]{2,1,0:T(8,128)(2,1)} %pad_maximum_fusion), calls=%async_computation.1 | async-start | bytes 524288 | tf_op jit(solution)/shard_map/all_to_all | solution.py:104
  52.9 7.4 %all-to-all-done.1 = bf16[16,8,1024]{2,1,0:T(8,128)(2,1)S(1)} async-done(((bf16[16,8,1024]{2,1,0:T(8,128)(2,1)}), bf16[16,8,1024]{2,1,0:T(8,128)(2,1)S(1)}, u32[]{:S(2)}, u32[]{:S(2)}) %all-to-all-start.1) | async-done | bytes 262176 | tf_op jit(solution)/shard_map/all_to_all | solution.py:104
  63.3 2.5 %fusion.3 = bf16[64,1024]{1,0:T(8,128)(2,1)} fusion(bf16[1,512,1024]{2,1,0:T(8,128)(2,1)} %param.16, bf16[1,1024,512]{2,1,0:T(8,128)(2,1)S(1)} %copy-done, f32[1024]{0:T(1024)S(1)} %bitcast.493, pred[]{:T(512)S(6)} %eq.6, bf16[16,8,1024]{2,1,0:T(8,128)(2,1)S(1)} %all-to-all-done.1, bf16[4,64,1024]{2,1,0:T(8,128)(2,1)S(1)} %copy-done.9, f32[64]{0:T(128)} %add_rsqrt_fusion.6), kind=kOutput, calls=%fused_computation.10 | convolution fusion | flops 135135232 | bytes 2757888 | tf_op jit(solution)/shard_map/dot_general | solution.py:74
  67.4 3.5 %all-to-all-start.2 = ((bf16[16,8,1024]{2,1,0:T(8,128)(2,1)}), bf16[16,8,1024]{2,1,0:T(8,128)(2,1)S(1)}, u32[]{:S(2)}, u32[]{:S(2)}) async-start(bf16[16,8,1024]{2,1,0:T(8,128)(2,1)} %maximum_bitcast_fusion.1), calls=%async_computation.2 | async-start | bytes 524288 | tf_op jit(solution)/shard_map/all_to_all | solution.py:98
  71.6 7.4 %all-to-all-done.2 = bf16[16,8,1024]{2,1,0:T(8,128)(2,1)S(1)} async-done(((bf16[16,8,1024]{2,1,0:T(8,128)(2,1)}), bf16[16,8,1024]{2,1,0:T(8,128)(2,1)S(1)}, u32[]{:S(2)}, u32[]{:S(2)}) %all-to-all-start.2) | async-done | bytes 262176 | tf_op jit(solution)/shard_map/all_to_all | solution.py:98
  79.8 7.2 %all-to-all-start.3 = ((bf16[16,8,1024]{2,1,0:T(8,128)(2,1)}), bf16[16,8,1024]{2,1,0:T(8,128)(2,1)S(1)}, u32[]{:S(2)}, u32[]{:S(2)}) async-start(bf16[16,8,1024]{2,1,0:T(8,128)(2,1)} %pad_maximum_fusion.1), calls=%async_computation.3 | async-start | bytes 524288 | tf_op jit(solution)/shard_map/all_to_all | solution.py:104
  88.1 6.7 %all-to-all-done.3 = bf16[16,8,1024]{2,1,0:T(8,128)(2,1)S(1)} async-done(((bf16[16,8,1024]{2,1,0:T(8,128)(2,1)}), bf16[16,8,1024]{2,1,0:T(8,128)(2,1)S(1)}, u32[]{:S(2)}, u32[]{:S(2)}) %all-to-all-start.3) | async-done | bytes 262176 | tf_op jit(solution)/shard_map/all_to_all | solution.py:104
  98.3 2.5 %fusion.4 = bf16[64,1024]{1,0:T(8,128)(2,1)} fusion(bf16[1,512,1024]{2,1,0:T(8,128)(2,1)} %param.16, bf16[1,1024,512]{2,1,0:T(8,128)(2,1)S(1)} %copy-done, f32[1024]{0:T(1024)S(1)} %bitcast.498, pred[]{:T(512)S(6)} %eq.6, bf16[16,8,1024]{2,1,0:T(8,128)(2,1)S(1)} %all-to-all-done.3, bf16[4,64,1024]{2,1,0:T(8,128)(2,1)} %param.11, f32[64]{0:T(128)S(1)} %add_rsqrt_fusion.4), kind=kOutput, calls=%fused_computation.11 | convolution fusion | flops 135135232 | bytes 2757888 | tf_op jit(solution)/shard_map/dot_general | solution.py:74
  102.4 3.7 %all-to-all-start.4 = ((bf16[16,8,1024]{2,1,0:T(8,128)(2,1)}), bf16[16,8,1024]{2,1,0:T(8,128)(2,1)S(1)}, u32[]{:S(2)}, u32[]{:S(2)}) async-start(bf16[16,8,1024]{2,1,0:T(8,128)(2,1)} %maximum_bitcast_fusion.2), calls=%async_computation.4 | async-start | bytes 524288 | tf_op jit(solution)/shard_map/all_to_all | solution.py:98
  108.8 5.3 %all-to-all-done.4 = bf16[16,8,1024]{2,1,0:T(8,128)(2,1)S(1)} async-done(((bf16[16,8,1024]{2,1,0:T(8,128)(2,1)}), bf16[16,8,1024]{2,1,0:T(8,128)(2,1)S(1)}, u32[]{:S(2)}, u32[]{:S(2)}) %all-to-all-start.4) | async-done | bytes 262176 | tf_op jit(solution)/shard_map/all_to_all | solution.py:98
  115.0 7.3 %all-to-all-start.5 = ((bf16[16,8,1024]{2,1,0:T(8,128)(2,1)}), bf16[16,8,1024]{2,1,0:T(8,128)(2,1)S(1)}, u32[]{:S(2)}, u32[]{:S(2)}) async-start(bf16[16,8,1024]{2,1,0:T(8,128)(2,1)} %pad_maximum_fusion.2), calls=%async_computation.5 | async-start | bytes 524288 | tf_op jit(solution)/shard_map/all_to_all | solution.py:104
  124.9 5.1 %all-to-all-done.5 = bf16[16,8,1024]{2,1,0:T(8,128)(2,1)S(1)} async-done(((bf16[16,8,1024]{2,1,0:T(8,128)(2,1)}), bf16[16,8,1024]{2,1,0:T(8,128)(2,1)S(1)}, u32[]{:S(2)}, u32[]{:S(2)}) %all-to-all-start.5) | async-done | bytes 262176 | tf_op jit(solution)/shard_map/all_to_all | solution.py:104
  134.0 2.5 %fusion.5 = bf16[64,1024]{1,0:T(8,128)(2,1)} fusion(bf16[1,512,1024]{2,1,0:T(8,128)(2,1)} %param.16, bf16[1,1024,512]{2,1,0:T(8,128)(2,1)S(1)} %copy-done, f32[1024]{0:T(1024)S(1)} %bitcast.504, pred[]{:T(512)S(6)} %eq.6, bf16[16,8,1024]{2,1,0:T(8,128)(2,1)S(1)} %all-to-all-done.5, bf16[4,64,1024]{2,1,0:T(8,128)(2,1)} %param.11, f32[64]{0:T(128)S(1)} %add_rsqrt_fusion.2), kind=kOutput, calls=%fused_computation.12 | convolution fusion | flops 135135232 | bytes 2757888 | tf_op jit(solution)/shard_map/dot_general | solution.py:74
  138.2 4.2 %all-to-all-start.6 = ((bf16[16,8,1024]{2,1,0:T(8,128)(2,1)}), bf16[16,8,1024]{2,1,0:T(8,128)(2,1)}, u32[]{:S(2)}, u32[]{:S(2)}) async-start(bf16[16,8,1024]{2,1,0:T(8,128)(2,1)} %maximum_bitcast_fusion.3), calls=%async_computation.6 | async-start | bytes 524288 | tf_op jit(solution)/shard_map/all_to_all | solution.py:98
  146.2 4.3 %all-to-all-done.6 = bf16[16,8,1024]{2,1,0:T(8,128)(2,1)} async-done(((bf16[16,8,1024]{2,1,0:T(8,128)(2,1)}), bf16[16,8,1024]{2,1,0:T(8,128)(2,1)}, u32[]{:S(2)}, u32[]{:S(2)}) %all-to-all-start.6) | async-done | bytes 262176 | tf_op jit(solution)/shard_map/all_to_all | solution.py:98
  152.3 7.0 %all-to-all-start.7 = ((bf16[16,8,1024]{2,1,0:T(8,128)(2,1)}), bf16[16,8,1024]{2,1,0:T(8,128)(2,1)}, u32[]{:S(2)}, u32[]{:S(2)}) async-start(bf16[16,8,1024]{2,1,0:T(8,128)(2,1)} %pad_maximum_fusion.3), calls=%async_computation.7 | async-start | bytes 524288 | tf_op jit(solution)/shard_map/all_to_all | solution.py:104
  163.5 3.6 %all-to-all-done.7 = bf16[16,8,1024]{2,1,0:T(8,128)(2,1)} async-done(((bf16[16,8,1024]{2,1,0:T(8,128)(2,1)}), bf16[16,8,1024]{2,1,0:T(8,128)(2,1)}, u32[]{:S(2)}, u32[]{:S(2)}) %all-to-all-start.7) | async-done | bytes 262176 | tf_op jit(solution)/shard_map/all_to_all | solution.py:104
  169.0 2.4 %fusion.81 = (f32[1024]{0:T(1024)S(1)}, f32[1024]{0:T(1024)S(1)}, f32[1024]{0:T(1024)S(1)}, f32[1024]{0:T(1024)S(1)}, f32[1024]{0:T(1024)S(1)}, /*index=5*/bf16[8,8,1024]{2,1,0:T(8,128)(2,1)}, f32[64]{0:T(128)S(1)}) fusion(f32[64,1024]{1,0:T(8,128)S(1)} %get-tuple-element.55, bf16[1,5,64,1024]{3,2,1,0:T(8,128)(2,1)S(1)} %copy-done.1, s32[]{:T(128)S(6)} %select_n.94, ...), kind=kOutput, calls=%fused_computation.115 | convolution fusion | flops 68938688 | bytes 3564310 | tf_op jit(solution)/shard_map/dot_general | solution.py:20
  174.6 3.5 %all-to-all-start.8 = ((bf16[8,24,1024]{2,1,0:T(8,128)(2,1)}), bf16[8,24,1024]{2,1,0:T(8,128)(2,1)S(1)}, u32[]{:S(2)}, u32[]{:S(2)}) async-start(bf16[8,24,1024]{2,1,0:T(8,128)(2,1)} %maximum_maximum_fusion), calls=%async_computation.8 | async-start | bytes 786432 | tf_op jit(solution)/shard_map/all_to_all | solution.py:120
  179.9 5.6 %all-to-all-done.8 = bf16[8,24,1024]{2,1,0:T(8,128)(2,1)S(1)} async-done(((bf16[8,24,1024]{2,1,0:T(8,128)(2,1)}), bf16[8,24,1024]{2,1,0:T(8,128)(2,1)S(1)}, u32[]{:S(2)}, u32[]{:S(2)}) %all-to-all-start.8) | async-done | bytes 393248 | tf_op jit(solution)/shard_map/all_to_all | solution.py:120
  186.3 4.0 %all-to-all-start.9 = ((bf16[8,16,1024]{2,1,0:T(8,128)(2,1)}), bf16[8,16,1024]{2,1,0:T(8,128)(2,1)S(1)}, u32[]{:S(2)}, u32[]{:S(2)}) async-start(bf16[8,16,1024]{2,1,0:T(8,128)(2,1)} %broadcast_in_dim.38), calls=%async_computation.9 | async-start | bytes 524288 | tf_op jit(solution)/shard_map/all_to_all | solution.py:123
  190.3 2.7 %fusion = bf16[1,1024,512]{2,1,0:T(8,128)(2,1)} fusion(bf16[320,1024]{1,0:T(8,128)(2,1)S(1)} %copy-done.8, bf16[320,512]{1,0:T(8,128)(2,1)} %get-tuple-element.35), kind=kOutput, calls=%fused_computation.2 | convolution fusion | flops 336068608 | bytes 2031616 | tf_op jit(solution)/shard_map/dot_general | solution.py:26
  193.0 2.7 %fusion.1 = bf16[1,512,1024]{2,1,0:T(8,128)(2,1)} fusion(bf16[320,512]{1,0:T(8,128)(2,1)} %get-tuple-element.34, bf16[320,1024]{1,0:T(8,128)(2,1)S(1)} %constant_dynamic-update-slice_fusion.5), kind=kOutput, calls=%fused_computation.3 | convolution fusion | flops 336068608 | bytes 2031616 | tf_op jit(solution)/shard_map/dot_general | solution.py:26
  (146 shorter events, 53.3 us)
Async XLA Ops:
  0.6 15.1 %copy-start = (bf16[1,1024,512]{2,1,0:T(8,128)(2,1)S(1)}, bf16[1,1024,512]{2,1,0:T(8,128)(2,1)}, u32[]{:S(2)}) copy-start(bf16[1,1024,512]{2,1,0:T(8,128)(2,1)} %param.15) | copy-start | bytes 3145732
  8.6 8.3 %copy-start.5 = (bf16[1,512,1024]{2,1,0:T(8,128)(2,1)S(1)}, bf16[1,512,1024]{2,1,0:T(8,128)(2,1)}, u32[]{:S(2)}) copy-start(bf16[1,512,1024]{2,1,0:T(8,128)(2,1)} %param.16) | copy-start | bytes 3145732
  8.6 8.3 %copy-start.25 = (bf16[1,64,1024]{2,1,0:T(8,128)(2,1)S(1)}, bf16[1,64,1024]{2,1,0:T(8,128)(2,1)}, u32[]{:S(2)}) copy-start(bf16[1,64,1024]{2,1,0:T(8,128)(2,1)} %param.9) | copy-start | bytes 393220
  36.8 23.5 %copy-start.2 = (bf16[4,64,1024]{2,1,0:T(8,128)(2,1)S(1)}, bf16[4,64,1024]{2,1,0:T(8,128)(2,1)}, u32[]{:S(2)}) copy-start(bf16[4,64,1024]{2,1,0:T(8,128)(2,1)} %param.12) | copy-start | bytes 1572868
  36.8 23.5 %all-to-all-start.1 = ((bf16[16,8,1024]{2,1,0:T(8,128)(2,1)}), bf16[16,8,1024]{2,1,0:T(8,128)(2,1)S(1)}, u32[]{:S(2)}, u32[]{:S(2)}) async-start(bf16[16,8,1024]{2,1,0:T(8,128)(2,1)} %pad_maximum_fusion), calls=%async_computation.1 | async-start | bytes 524288 | tf_op jit(solution)/shard_map/all_to_all | solution.py:104
  52.9 9.3 %copy-start.10 = (f32[64,512]{1,0:T(8,128)}, f32[64,512]{1,0:T(8,128)S(1)}, u32[]{:S(2)}) copy-start(f32[64,512]{1,0:T(8,128)S(1)} %fusion.26) | copy-start | bytes 393220
  52.9 9.3 %copy-start.9 = (bf16[4,64,1024]{2,1,0:T(8,128)(2,1)S(1)}, bf16[4,64,1024]{2,1,0:T(8,128)(2,1)}, u32[]{:S(2)}) copy-start(bf16[4,64,1024]{2,1,0:T(8,128)(2,1)} %param.11) | copy-start | bytes 1572868
  67.4 11.6 %all-to-all-start.2 = ((bf16[16,8,1024]{2,1,0:T(8,128)(2,1)}), bf16[16,8,1024]{2,1,0:T(8,128)(2,1)S(1)}, u32[]{:S(2)}, u32[]{:S(2)}) async-start(bf16[16,8,1024]{2,1,0:T(8,128)(2,1)} %maximum_bitcast_fusion.1), calls=%async_computation.2 | async-start | bytes 524288 | tf_op jit(solution)/shard_map/all_to_all | solution.py:98
  79.8 15.0 %all-to-all-start.3 = ((bf16[16,8,1024]{2,1,0:T(8,128)(2,1)}), bf16[16,8,1024]{2,1,0:T(8,128)(2,1)S(1)}, u32[]{:S(2)}, u32[]{:S(2)}) async-start(bf16[16,8,1024]{2,1,0:T(8,128)(2,1)} %pad_maximum_fusion.1), calls=%async_computation.3 | async-start | bytes 524288 | tf_op jit(solution)/shard_map/all_to_all | solution.py:104
  88.0 8.7 %copy-start.14 = (f32[64,512]{1,0:T(8,128)}, f32[64,512]{1,0:T(8,128)S(1)}, u32[]{:S(2)}) copy-start(f32[64,512]{1,0:T(8,128)S(1)} %fusion.21) | copy-start | bytes 393220
  102.4 11.7 %all-to-all-start.4 = ((bf16[16,8,1024]{2,1,0:T(8,128)(2,1)}), bf16[16,8,1024]{2,1,0:T(8,128)(2,1)S(1)}, u32[]{:S(2)}, u32[]{:S(2)}) async-start(bf16[16,8,1024]{2,1,0:T(8,128)(2,1)} %maximum_bitcast_fusion.2), calls=%async_computation.4 | async-start | bytes 524288 | tf_op jit(solution)/shard_map/all_to_all | solution.py:98
  115.0 15.0 %all-to-all-start.5 = ((bf16[16,8,1024]{2,1,0:T(8,128)(2,1)}), bf16[16,8,1024]{2,1,0:T(8,128)(2,1)S(1)}, u32[]{:S(2)}, u32[]{:S(2)}) async-start(bf16[16,8,1024]{2,1,0:T(8,128)(2,1)} %pad_maximum_fusion.2), calls=%async_computation.5 | async-start | bytes 524288 | tf_op jit(solution)/shard_map/all_to_all | solution.py:104
  122.9 8.9 %copy-start.26 = (f32[64]{0:T(128)}, f32[64]{0:T(128)S(1)}, u32[]{:S(2)}) copy-start(f32[64]{0:T(128)S(1)} %add_rsqrt_fusion.3) | copy-start | bytes 772
  124.9 7.0 %copy-start.17 = (f32[64,512]{1,0:T(8,128)}, f32[64,512]{1,0:T(8,128)S(1)}, u32[]{:S(2)}) copy-start(f32[64,512]{1,0:T(8,128)S(1)} %fusion.16) | copy-start | bytes 393220
  124.9 6.9 %copy-start.30 = (f32[64]{0:T(128)S(1)}, f32[64]{0:T(128)}, u32[]{:S(2)}) copy-start(f32[64]{0:T(128)} %get-tuple-element.14) | copy-start | bytes 772
  138.2 12.3 %all-to-all-start.6 = ((bf16[16,8,1024]{2,1,0:T(8,128)(2,1)}), bf16[16,8,1024]{2,1,0:T(8,128)(2,1)}, u32[]{:S(2)}, u32[]{:S(2)}) async-start(bf16[16,8,1024]{2,1,0:T(8,128)(2,1)} %maximum_bitcast_fusion.3), calls=%async_computation.6 | async-start | bytes 524288 | tf_op jit(solution)/shard_map/all_to_all | solution.py:98
  145.4 13.9 %copy-start.4 = (bf16[16,8,1024]{2,1,0:T(8,128)(2,1)S(1)}, bf16[16,8,1024]{2,1,0:T(8,128)(2,1)}, u32[]{:S(2)}) copy-start(bf16[16,8,1024]{2,1,0:T(8,128)(2,1)} %copy-done.3) | copy-start | bytes 786436
  151.5 10.2 %copy-start.27 = (f32[64]{0:T(128)S(1)}, f32[64]{0:T(128)}, u32[]{:S(2)}) copy-start(f32[64]{0:T(128)} %copy-done.26) | copy-start | bytes 772
  152.3 14.8 %all-to-all-start.7 = ((bf16[16,8,1024]{2,1,0:T(8,128)(2,1)}), bf16[16,8,1024]{2,1,0:T(8,128)(2,1)}, u32[]{:S(2)}, u32[]{:S(2)}) async-start(bf16[16,8,1024]{2,1,0:T(8,128)(2,1)} %pad_maximum_fusion.3), calls=%async_computation.7 | async-start | bytes 524288 | tf_op jit(solution)/shard_map/all_to_all | solution.py:104
  161.7 7.3 %copy-start.29 = (f32[64]{0:T(128)S(1)}, f32[64]{0:T(128)}, u32[]{:S(2)}) copy-start(f32[64]{0:T(128)} %get-tuple-element.10) | copy-start | bytes 772
  161.7 7.3 %copy-start.6 = (f32[64,1024]{1,0:T(8,128)S(1)}, f32[64,1024]{1,0:T(8,128)}, u32[]{:S(2)}) copy-start(f32[64,1024]{1,0:T(8,128)} %get-tuple-element.52) | copy-start | bytes 786436
  174.6 11.0 %all-to-all-start.8 = ((bf16[8,24,1024]{2,1,0:T(8,128)(2,1)}), bf16[8,24,1024]{2,1,0:T(8,128)(2,1)S(1)}, u32[]{:S(2)}, u32[]{:S(2)}) async-start(bf16[8,24,1024]{2,1,0:T(8,128)(2,1)} %maximum_maximum_fusion), calls=%async_computation.8 | async-start | bytes 786432 | tf_op jit(solution)/shard_map/all_to_all | solution.py:120
  178.1 12.2 %copy-start.8 = (bf16[320,1024]{1,0:T(8,128)(2,1)S(1)}, bf16[320,1024]{1,0:T(8,128)(2,1)}, u32[]{:S(2)}) copy-start(bf16[320,1024]{1,0:T(8,128)(2,1)} %fusion.222) | copy-start | bytes 1966084
  186.3 10.1 %all-to-all-start.9 = ((bf16[8,16,1024]{2,1,0:T(8,128)(2,1)}), bf16[8,16,1024]{2,1,0:T(8,128)(2,1)S(1)}, u32[]{:S(2)}, u32[]{:S(2)}) async-start(bf16[8,16,1024]{2,1,0:T(8,128)(2,1)} %broadcast_in_dim.38), calls=%async_computation.9 | async-start | bytes 524288 | tf_op jit(solution)/shard_map/all_to_all | solution.py:123
  (17 other events, 48.8 us)

commit v2 on v1

v2 whole, which is shorter than its diff:
```python
import jax
import jax.numpy as jnp
from jax import lax
from jax.experimental import pallas as pl
from jax.experimental.pallas import tpu as pltpu
from jax.sharding import PartitionSpec as P

D = 1024
EPSILON = 1e-06
BOTH = ("section", "mp")
BF16 = jnp.bfloat16
F32 = jnp.float32
LANES = 128
VMEM_LIMIT = 8 << 20
ROOT = 0.7978845608028654
CUBE = 0.044715


def pair_groups(sections, peers, first):
    groups = []
    for k in range(first, sections + first, 2):
        pair = (k % sections, (k + 1) % sections)
        groups.append([s * peers + m for s in pair for m in range(peers)])
    return groups


def times(left, right):
    return jnp.dot(left, right, preferred_element_type=F32)


def against_rows(left, right):
    return lax.dot_general(left, right, (((1,), (1,)), ((), ())), preferred_element_type=F32)


def across_rows(left, right):
    return lax.dot_general(left, right, (((0,), (0,)), ((), ())), preferred_element_type=F32)


def in_vmem(value):
    return pltpu.with_memory_space_constraint(value, pltpu.VMEM)


def call(kernel, outs, args, flops, smem=(), hbm=(), scratch=()):
    space = lambda k: pltpu.SMEM if k in smem else pltpu.HBM if k in hbm else pltpu.VMEM
    return pl.pallas_call(
        kernel,
        out_shape=[
            {"vmem": pltpu.VMEM, "hbm": pltpu.HBM, "any": jax.ShapeDtypeStruct}[place](shape, dtype)
            for shape, dtype, place in outs
        ],
        in_specs=[pl.BlockSpec(memory_space=space(k)) for k in range(len(args))],
        out_specs=[
            pl.BlockSpec(memory_space=pltpu.HBM if place == "hbm" else pltpu.VMEM) for _, _, place in outs
        ],
        scratch_shapes=list(scratch),
        compiler_params=pltpu.CompilerParams(vmem_limit_bytes=VMEM_LIMIT),
        cost_estimate=pl.CostEstimate(flops=flops, transcendentals=0, bytes_accessed=1 << 20),
    )(*args)


def normalize(rows, gain, weight_in):
    scaled = (rows * gain).astype(BF16)
    inverse = lax.rsqrt(jnp.sum(rows * rows, axis=1, keepdims=True) * (1.0 / D) + EPSILON)
    return scaled, inverse, times(scaled, weight_in)


def gelu_parts(preact):
    square = preact * preact
    tanh = jnp.tanh(ROOT * preact * (1.0 + CUBE * square))
    cdf = 0.5 + 0.5 * tanh
    return preact * cdf, cdf, tanh, square


def gelu_slope(preact, cdf, tanh, square):
    return cdf + (0.5 * ROOT) * preact * (1.0 - tanh * tanh) * (1.0 + (3.0 * CUBE) * square)


def flat(ref, peers, start):
    part = ref[start : start + peers].astype(F32)
    return part.reshape(part.shape[0] * part.shape[1], part.shape[2])


def step_kernel(peers, step, last, *refs):
    refs = list(refs)
    take = lambda count: [refs.pop(0) for _ in range(count)]
    plan, stashed = take(2)
    sources = take(1 if step else 2)
    gain_ref, weight_in, weight_out = take(3)
    gains = take(step if last else 0)
    (parts_out,) = take(1)
    targets = take(4 if last else 5)
    slot_ref, *kept = take(6)
    gains_kept = take(len(gains))
    (sems,) = take(1)

    fetches = [pltpu.make_async_copy(stashed.at[plan[0, step]], slot_ref, sems.at[0])]
    fetches += [
        pltpu.make_async_copy(ref, target, sems.at[6 + k]) for k, (ref, target) in enumerate(zip(gains, gains_kept))
    ]
    for fetch in fetches:
        fetch.start()
    stores = [pltpu.make_async_copy(ref, target, sems.at[1 + k]) for k, (ref, target) in enumerate(zip(kept, targets))]

    def keep(which, value):
        kept[which][...] = value
        stores[which].start()

    if step:
        inputs, grads = flat(sources[0], peers, 0), flat(sources[0], peers, peers)
        grads_low = grads.astype(BF16)
    else:
        inputs, grads_low = sources[0][...].astype(F32), sources[1][...]
        grads = grads_low.astype(F32)
    keep(2, grads_low)
    gain = gain_ref[...].astype(F32)
    portion = 1.0 / peers
    share = inputs.shape[0] // peers

    hidden_grad = against_rows(grads_low, weight_out[...])
    _, inverse, projected = normalize(inputs, gain, weight_in[...])

    fetches[0].wait()
    slot = slot_ref[...].astype(F32)
    slot_scaled, slot_inverse, slot_projected = normalize(slot, gain, weight_in[...])
    keep(1, slot_scaled)

    hidden = gelu_parts(inverse * projected)[0].astype(BF16)
    forward = times(hidden, weight_out[...]) + inputs * portion

    slot_preact = slot_inverse * slot_projected
    slot_hidden, *about = gelu_parts(slot_preact)
    keep(0, slot_hidden.astype(BF16))
    pre_grad = hidden_grad * gelu_slope(slot_preact, *about)
    update = (slot_inverse * pre_grad).astype(BF16)
    keep(3, update)
    input_part = against_rows(update, weight_in[...])
    inner = jnp.sum(pre_grad * slot_projected, axis=1, keepdims=True)
    factor = inner * slot_inverse * slot_inverse * slot_inverse * (-1.0 / D)
    gain_sum = jnp.sum(input_part * slot, axis=0, keepdims=True)
    backward = grads * portion + input_part * gain + factor * slot

    forward = forward.reshape(peers, share, D).astype(BF16)
    backward = backward.reshape(peers, share, D).astype(BF16)
    if last:
        parts_out[:peers, :, :D] = forward
        parts_out[peers:, :, :D] = backward
        for fetch, ref in zip(fetches[1:], gains_kept):
            fetch.wait()
            gain_sum = gain_sum + ref[...]
        stack = jnp.concatenate([gain_sum[:, k * LANES : (k + 1) * LANES] for k in range(D // LANES)], axis=0)
        high = stack.astype(BF16)
        low = (stack - high.astype(F32)).astype(BF16)
        for k in range(2 * peers):
            parts_out[k, :, D : D + LANES] = high
            parts_out[k, :, D + LANES :] = low
    else:
        keep(4, gain_sum)
        parts_out[:peers] = backward
        parts_out[peers:] = forward
    for store in stores:
        store.wait()


def sum_kernel(peers, sections, step, received, feed_rows, feed_grads, spread_out):
    position = lax.axis_index("section")
    for start, edge, feed in ((0, 0, feed_rows), (peers, sections - 1, feed_grads)):
        total = received[start].astype(F32)
        for k in range(1, peers):
            total = total + received[start + k].astype(F32)
        total = jnp.where(position == edge, feed[step].astype(F32), total).astype(BF16)
        for k in range(peers):
            spread_out[start + k] = total


def last_sum_kernel(peers, received, spread_out, gain_out):
    for start in (0, peers):
        total = received[start, :, :D].astype(F32)
        for k in range(1, peers):
            total = total + received[start + k, :, :D].astype(F32)
        total = total.astype(BF16)
        for k in range(peers):
            spread_out[start + k] = total
    own = lax.rem(lax.axis_index("section"), 2) * peers
    total = jnp.zeros((D // LANES, LANES), F32)
    for k in range(peers):
        total = total + received[own + k, :, D : D + LANES].astype(F32)
        total = total + received[own + k, :, D + LANES :].astype(F32)
    gain_out[...] = total


def update_kernel(steps, *refs):
    out, left, right = refs[-3:]
    rows = refs[0].shape[0]
    for step in range(steps):
        left[step * rows : (step + 1) * rows, :] = refs[step][...]
        right[step * rows : (step + 1) * rows, :] = refs[steps + step][...]
    out[...] = across_rows(left[...], right[...]).astype(BF16)


def finish_kernel(peers, received, outputs, input_grad):
    outputs[...] = flat(received, peers, 0).astype(BF16)
    input_grad[...] = flat(received, peers, peers).astype(BF16)


def local(
    arrive_rows,
    arrive_grads,
    feed_rows,
    feed_grads,
    stashed_rows,
    slot_order,
    enter_weight,
    leave_weight,
    norm_gain,
):
    sections = lax.axis_size("section")
    peers = lax.axis_size("mp")
    even_pairs = pair_groups(sections, peers, 0)
    odd_pairs = pair_groups(sections, peers, 1)
    weight_in = in_vmem(enter_weight[0])
    weight_out = in_vmem(leave_weight[0])
    gain = in_vmem(norm_gain)
    stashed = pltpu.with_memory_space_constraint(stashed_rows[0], pltpu.HBM)
    steps, rows = stashed.shape[0], stashed.shape[1]
    width = enter_weight.shape[2]
    share = rows // peers
    matmul = 2 * rows * D * width
    own = lax.axis_index("mp") * share
    feeds = [in_vmem(lax.dynamic_slice_in_dim(feed, own, share, 1)) for feed in (feed_rows, feed_grads)]

    def exchange(parts, groups):
        return in_vmem(lax.all_to_all(parts, BOTH, 0, 0, axis_index_groups=groups, tiled=True))

    def spread(kernel, more, *args):
        outs = [((2 * peers, share, D), BF16, "vmem")] + more
        return call(kernel, outs, args, 1 << 18)

    kept = [((rows, width), BF16), ((rows, D), BF16), ((rows, D), BF16), ((rows, width), BF16), ((1, D), F32)]
    source = (in_vmem(arrive_rows[0]), in_vmem(arrive_grads[0]))
    stored = [[] for _ in kept]
    for step in range(steps):
        last = step + 1 == steps
        gains = stored[4] if last else []
        args = [slot_order, stashed, *source, gain, weight_in, weight_out, *gains]
        outs = [((2 * peers, share, D + 2 * LANES if last else D), BF16, "vmem")]
        outs += [(shape, dtype, "hbm") for shape, dtype in kept[: 4 if last else 5]]
        scratch = [pltpu.VMEM((rows, D), BF16), *(pltpu.VMEM(*k) for k in kept), *(pltpu.VMEM((1, D), F32) for _ in gains)]
        scratch.append(pltpu.SemaphoreType.DMA((6 + steps,)))
        kernel = lambda *refs: step_kernel(peers, step, last, *refs)
        in_hbm = [1, *range(len(args) - len(gains), len(args))]
        parts, *results = call(kernel, outs, args, 5 * matmul, smem=(0,), hbm=in_hbm, scratch=scratch)
        for past, result in zip(stored, results):
            past.append(result)
        if last:
            break
        (parts,) = spread(
            lambda *refs: sum_kernel(peers, sections, step, *refs), [], exchange(parts, odd_pairs), *feeds
        )
        source = (exchange(parts, even_pairs),)

    parts, gain_total = spread(
        lambda *refs: last_sum_kernel(peers, *refs),
        [((D // LANES, LANES), F32, "any")],
        exchange(parts, even_pairs),
    )
    received = exchange(parts, even_pairs)
    kernel = lambda *refs: finish_kernel(peers, *refs)
    outputs, input_grad = call(kernel, [((rows, D), BF16, "any")] * 2, (received,), 1 << 18)
    totals = []
    for left, right in ((stored[0], stored[2]), (stored[1], stored[3])):
        shape = (left[0].shape[1], right[0].shape[1])
        scratch = [pltpu.VMEM((steps * rows, n), BF16) for n in shape]
        kernel = lambda *refs: update_kernel(steps, *refs)
        totals += call(kernel, [(shape, BF16, "any")], (*left, *right), steps * matmul, scratch=scratch)
    return (
        outputs[None],
        input_grad[None],
        totals[1][None],
        totals[0][None],
        gain_total.reshape(1, D),
    )


def solution(mesh):
    placed = (
        P("section", None, None),
        P("section", None, None),
        P(),
        P(),
        P("section", None, None, None),
        P("section", None),
        P("section", None, "mp"),
        P("section", "mp", None),
        P("section", None),
    )
    return jax.shard_map(
        local,
        mesh=mesh,
        in_specs=placed,
        out_specs=(
            P("section", None, None),
            P("section", None, None),
            P("section", None, "mp"),
            P("section", "mp", None),
            P("section", None),
        ),
        check_vma=False,
    )
```

time: 199 us -> 165 us (0.83)
  blocking collectives: 15.9 us -> 113 us
  starting transfers between devices: 56.1 us -> 12.1 us
  waiting for transfers between devices: 45.6 us -> 11 us
  matrix products: 34.2 us -> 0 us
  other arithmetic: 28.9 us -> 0 us
  Pallas kernels: 0 us -> 20.6 us
  between operations: 11.1 us -> 1 us
    all_to_all x1 -> x8, blocking collectives: 15.9 us -> 113 us  [exchange(): lax.all_to_all(parts, BOTH, 0, 0, axis_index_groups=groups, tiled=True)]
    all_to_all x9 -> x2, starting transfers between devices: 56.1 us -> 12.1 us  [exchange(): lax.all_to_all(parts, BOTH, 0, 0, axis_index_groups=groups, tiled=True)]
    all_to_all x9 -> x2, waiting for transfers between devices: 45.6 us -> 11 us  [exchange(): lax.all_to_all(parts, BOTH, 0, 0, axis_index_groups=groups, tiled=True)]
    dot_general x22 -> x0, matrix products: 34.2 us -> none  [the longest x10 15.7 us: against_rows(): lax.dot_general(left, right, (((1,), (1,)), ((), ())), preferred_element_...]
    pallas_call x0 -> x13, Pallas kernels: none -> 20.6 us  [call(): pl.pallas_call(kernel, out_shape=[{'vmem': pltpu.VMEM, 'hbm': pltpu.HBM,...]
    unnamed x11 -> x0, other arithmetic: 10.1 us -> none
    concatenate x8 -> x0, other arithmetic: 6.26 us -> none  [the longest x4 2.93 us: local(): jnp.concatenate([jnp.broadcast_to(low[None], spread), jnp.broadcast_to(hi...]
    reshape x4 -> x0, other arithmetic: 4.95 us -> none  [local(): jnp.concatenate([backward, forward], axis=0).reshape(2 * peers, share, D)]
  transfers between devices with their start and end apart: 9 -> 2, of which waited for: 9 -> 2; matrix products, arithmetic and copies ran while one was open for 12% -> 1% of each run, Pallas kernels for 0% -> 2%
where the time goes in v2:
time: 165 us; the launch traced here: 164 us
  blocking collectives  113 us (68%)
  Pallas kernels  20.6 us (12%)
  starting transfers between devices  12.1 us (7%)
  waiting for transfers between devices  11 us (7%)
  local copies, waits for them, and re-layouts  6.6 us (4%)
    all_to_all x8, blocking collectives, exchange(): lax.all_to_all(parts, BOTH, 0, 0, axis_index_groups=groups, tiled=True)  113 us
    pallas_call x13, Pallas kernels, call(): pl.pallas_call(kernel, out_shape=[{'vmem': pltpu.VMEM, 'hbm': pltpu.HBM,...  20.6 us
    all_to_all x2, starting transfers between devices, exchange(): lax.all_to_all(parts, BOTH, 0, 0, axis_index_groups=groups, tiled=True)  12.1 us
    all_to_all x2, waiting for transfers between devices, exchange(): lax.all_to_all(parts, BOTH, 0, 0, axis_index_groups=groups, tiled=True)  11 us
    unnamed x64, local copies, waits for them, and re-layouts  5.71 us
  transfers between devices with their start and end apart: 2, of which 2 were waited for; matrix products, arithmetic and copies ran while one was open for 1% of the time, Pallas kernels for 2%

profile of v2, /device:TPU:1, one launch (start us, length us, event | category | flops | bytes accessed | tf_op | source)
XLA Modules:
  0.0 164.3 jit_solution(13197385466755730989)
XLA Ops:
  1.3 1.2 copy-done
  2.6 1.2 copy-done.2
  3.8 0.9 copy-done.4
  4.7 0.9 copy-done.5
  5.6 3.8 %shard_map.128 = (bf16[16,8,1024]{2,1,0:T(8,128)(2,1)}, bf16[64,512]{1,0:T(8,128)(2,1)}, bf16[64,1024]{1,0:T(8,128)(2,1)}, bf16[64,1024]{1,0:T(8,128)(2,1)}, bf16[64,512]{1,0:T(8,128)(2,1)}, /*index=5*/f32[1,1024]{1,0:T(1,128)}) custom-call(s32[1,5]{1,0:T(1,128)S(1)} %copy-done.27, bf16[5,64,1024]{2,1,0:T(8,128)(2,1)} %bitcast.22, ...), custom_call_target="tpu_custom_call" | custom-call | flops 335544320 | bytes 1048576 | tf_op jit(solution)/shard_map/pallas_call | solution.py:45
  9.4 8.5 %all-to-all-start = ((bf16[16,8,1024]{2,1,0:T(8,128)(2,1)}), bf16[16,8,1024]{2,1,0:T(8,128)(2,1)S(1)}, u32[]{:S(2)}, u32[]{:S(2)}) async-start(bf16[16,8,1024]{2,1,0:T(8,128)(2,1)} %get-tuple-element.38), calls=%async_computation | async-start | bytes 524288 | tf_op jit(solution)/shard_map/all_to_all | solution.py:232
  17.8 0.9 constant_dynamic-slice_fusion
  18.7 6.9 %all-to-all-done.refs_0_ = bf16[16,8,1024]{2,1,0:T(8,128)(2,1)S(1)} async-done(((bf16[16,8,1024]{2,1,0:T(8,128)(2,1)}), bf16[16,8,1024]{2,1,0:T(8,128)(2,1)S(1)}, u32[]{:S(2)}, u32[]{:S(2)}) %all-to-all-start) | async-done | bytes 262176 | tf_op jit(solution)/shard_map/all_to_all | solution.py:232
  25.7 23.1 %all_to_all.50.refs_2_ = bf16[16,8,1024]{2,1,0:T(8,128)(2,1)S(1)} all-to-all(bf16[16,8,1024]{2,1,0:T(8,128)(2,1)S(1)} %shard_map.129), channel_id=1, replica_groups={{0,1,2,3,4,5,6,7,8,9,10,11,12,13,14,15},{16,17,18,19,20,21,22,23,24,25,..., dimensions={0} | all-to-all | bytes 524288 | tf_op jit(solution)/shard_map/all_to_all | solution.py:232
  48.8 3.0 %shard_map.130 = (bf16[16,8,1024]{2,1,0:T(8,128)(2,1)S(1)}, bf16[64,512]{1,0:T(8,128)(2,1)}, bf16[64,1024]{1,0:T(8,128)(2,1)}, bf16[64,1024]{1,0:T(8,128)(2,1)},...) custom-call(s32[1,5]{1,0:T(1,128)S(1)} %copy-done.27, bf16[5,64,1024]{2,1,0:T(8,128)(2,1)} %bitcast.23, ...), custom_call_target="tpu_custom_call" | custom-call | flops 335544320 | bytes 1048576 | tf_op jit(solution)/shard_map/pallas_call | solution.py:45
  51.9 10.7 %all_to_all.51.refs_0_ = bf16[16,8,1024]{2,1,0:T(8,128)(2,1)S(1)} all-to-all(bf16[16,8,1024]{2,1,0:T(8,128)(2,1)S(1)} %get-tuple-element.39), channel_id=1, replica_groups={{8,9,10,11,12,13,14,15,16,17,18,19,20,21,22,23},{24,25,26,27,28,29,30,3..., dimensions={0} | all-to-all | bytes 524288 | tf_op jit(solution)/shard_map/all_to_all | solution.py:232
  62.6 15.5 %all_to_all.52.refs_2_ = bf16[16,8,1024]{2,1,0:T(8,128)(2,1)S(1)} all-to-all(bf16[16,8,1024]{2,1,0:T(8,128)(2,1)S(1)} %shard_map.131), channel_id=1, replica_groups={{0,1,2,3,4,5,6,7,8,9,10,11,12,13,14,15},{16,17,18,19,20,21,22,23,24,25,..., dimensions={0} | all-to-all | bytes 524288 | tf_op jit(solution)/shard_map/all_to_all | solution.py:232
  78.1 3.0 %shard_map.132 = (bf16[16,8,1024]{2,1,0:T(8,128)(2,1)S(1)}, bf16[64,512]{1,0:T(8,128)(2,1)}, bf16[64,1024]{1,0:T(8,128)(2,1)}, bf16[64,1024]{1,0:T(8,128)(2,1)},...) custom-call(s32[1,5]{1,0:T(1,128)S(1)} %copy-done.27, bf16[5,64,1024]{2,1,0:T(8,128)(2,1)} %bitcast.24, ...), custom_call_target="tpu_custom_call" | custom-call | flops 335544320 | bytes 1048576 | tf_op jit(solution)/shard_map/pallas_call | solution.py:45
  81.1 10.7 %all_to_all.53.refs_0_ = bf16[16,8,1024]{2,1,0:T(8,128)(2,1)S(1)} all-to-all(bf16[16,8,1024]{2,1,0:T(8,128)(2,1)S(1)} %get-tuple-element.40), channel_id=1, replica_groups={{8,9,10,11,12,13,14,15,16,17,18,19,20,21,22,23},{24,25,26,27,28,29,30,3..., dimensions={0} | all-to-all | bytes 524288 | tf_op jit(solution)/shard_map/all_to_all | solution.py:232
  91.9 15.5 %all_to_all.54.refs_2_ = bf16[16,8,1024]{2,1,0:T(8,128)(2,1)S(1)} all-to-all(bf16[16,8,1024]{2,1,0:T(8,128)(2,1)S(1)} %shard_map.133), channel_id=1, replica_groups={{0,1,2,3,4,5,6,7,8,9,10,11,12,13,14,15},{16,17,18,19,20,21,22,23,24,25,..., dimensions={0} | all-to-all | bytes 524288 | tf_op jit(solution)/shard_map/all_to_all | solution.py:232
  107.3 3.0 %shard_map.134 = (bf16[16,8,1024]{2,1,0:T(8,128)(2,1)S(1)}, bf16[64,512]{1,0:T(8,128)(2,1)}, bf16[64,1024]{1,0:T(8,128)(2,1)}, bf16[64,1024]{1,0:T(8,128)(2,1)},...) custom-call(s32[1,5]{1,0:T(1,128)S(1)} %copy-done.27, bf16[5,64,1024]{2,1,0:T(8,128)(2,1)} %bitcast.25, ...), custom_call_target="tpu_custom_call" | custom-call | flops 335544320 | bytes 1048576 | tf_op jit(solution)/shard_map/pallas_call | solution.py:45
  110.4 10.7 %all_to_all.55.refs_0_ = bf16[16,8,1024]{2,1,0:T(8,128)(2,1)S(1)} all-to-all(bf16[16,8,1024]{2,1,0:T(8,128)(2,1)S(1)} %get-tuple-element.41), channel_id=1, replica_groups={{8,9,10,11,12,13,14,15,16,17,18,19,20,21,22,23},{24,25,26,27,28,29,30,3..., dimensions={0} | all-to-all | bytes 524288 | tf_op jit(solution)/shard_map/all_to_all | solution.py:232
  121.2 15.5 %all_to_all.56.refs_2_ = bf16[16,8,1024]{2,1,0:T(8,128)(2,1)S(1)} all-to-all(bf16[16,8,1024]{2,1,0:T(8,128)(2,1)S(1)} %shard_map.135), channel_id=1, replica_groups={{0,1,2,3,4,5,6,7,8,9,10,11,12,13,14,15},{16,17,18,19,20,21,22,23,24,25,..., dimensions={0} | all-to-all | bytes 524288 | tf_op jit(solution)/shard_map/all_to_all | solution.py:232
  137.3 2.6 %shard_map.136 = (bf16[16,8,1280]{2,1,0:T(8,128)(2,1)S(1)}, bf16[64,512]{1,0:T(8,128)(2,1)}, bf16[64,1024]{1,0:T(8,128)(2,1)}, bf16[64,1024]{1,0:T(8,128)(2,1)}, bf16[64,512]{1,0:T(8,128)(2,1)}) custom-call(s32[1,5]{1,0:T(1,128)S(1)} %copy-done.27, bf16[5,64,1024]{2,1,0:T(8,128)(2,1)} %bitcast.26, bf16[16,8,1024]{2,1,0:T(8,128)(2,1)S(1)} %all_to_all.56.refs_2_, ...), custom_call_target="tpu_custom_call" | custom-call | flops 335544320 | bytes 1048576 | tf_op jit(solution)/shard_map/pallas_call | solution.py:45
  140.0 11.5 %all_to_all.57.refs_0_ = bf16[16,8,1280]{2,1,0:T(8,128)(2,1)S(1)} all-to-all(bf16[16,8,1280]{2,1,0:T(8,128)(2,1)S(1)} %get-tuple-element.46), channel_id=1, replica_groups={{0,1,2,3,4,5,6,7,8,9,10,11,12,13,14,15},{16,17,18,19,20,21,22,23,24,25,..., dimensions={0} | all-to-all | bytes 655360 | tf_op jit(solution)/shard_map/all_to_all | solution.py:232
  152.2 3.6 %all-to-all-start.9 = ((bf16[16,8,1024]{2,1,0:T(8,128)(2,1)}), bf16[16,8,1024]{2,1,0:T(8,128)(2,1)S(1)}, u32[]{:S(2)}, u32[]{:S(2)}) async-start(bf16[16,8,1024]{2,1,0:T(8,128)(2,1)} %get-tuple-element.47), calls=%async_computation.9 | async-start | bytes 524288 | tf_op jit(solution)/shard_map/all_to_all | solution.py:232
  156.1 1.7 %shard_map.139 = bf16[1024,512]{1,0:T(8,128)(2,1)} custom-call(bf16[64,1024]{1,0:T(8,128)(2,1)S(1)} %copy-done.7, bf16[64,1024]{1,0:T(8,128)(2,1)S(1)} %copy-done.10, bf16[64,1024]{1,0:T(8,128)(2,1)S(1)} %copy-done.12, bf16[64,1024]{1,0:T(8,128)(2,1)S(1)} %copy-done.13, bf16[64,1024]{1,0:T(8,128)(2,1)S(1)} %copy-done.15, bf16[64,512]{1,0:T(8,128)(2,1)S(1)} %copy-done.18, ...), custom_call_target="tpu_custom_call" | custom-call | flops 335544320 | bytes 1048576 | tf_op jit(solution)/shard_map/pallas_call | solution.py:45
  157.9 1.7 %shard_map.140 = bf16[512,1024]{1,0:T(8,128)(2,1)} custom-call(bf16[64,512]{1,0:T(8,128)(2,1)S(1)} %copy-done.17, bf16[64,512]{1,0:T(8,128)(2,1)S(1)} %copy-done.19, bf16[64,512]{1,0:T(8,128)(2,1)S(1)} %copy-done.20, bf16[64,512]{1,0:T(8,128)(2,1)S(1)} %copy-done.22, bf16[64,512]{1,0:T(8,128)(2,1)S(1)} %copy-done.25, bf16[64,1024]{1,0:T(8,128)(2,1)S(1)} %copy-done.6, ...), custom_call_target="tpu_custom_call" | custom-call | flops 335544320 | bytes 1048576 | tf_op jit(solution)/shard_map/pallas_call | solution.py:45
  159.6 4.1 %all-to-all-done.9.refs_0_ = bf16[16,8,1024]{2,1,0:T(8,128)(2,1)S(1)} async-done(((bf16[16,8,1024]{2,1,0:T(8,128)(2,1)}), bf16[16,8,1024]{2,1,0:T(8,128)(2,1)S(1)}, u32[]{:S(2)}, u32[]{:S(2)}) %all-to-all-start.9) | async-done | bytes 262176 | tf_op jit(solution)/shard_map/all_to_all | solution.py:232
  (66 shorter events, 3.1 us)
Async XLA Ops:
  5.6 43.2 %copy-start.3 = (bf16[1,512,1024]{2,1,0:T(8,128)(2,1)S(1)}, bf16[1,512,1024]{2,1,0:T(8,128)(2,1)}, u32[]{:S(2)}) copy-start(bf16[1,512,1024]{2,1,0:T(8,128)(2,1)} %param.16) | copy-start | bytes 3145732
  9.3 39.5 %copy-start.1 = (bf16[1,1024,512]{2,1,0:T(8,128)(2,1)S(1)}, bf16[1,1024,512]{2,1,0:T(8,128)(2,1)}, u32[]{:S(2)}) copy-start(bf16[1,1024,512]{2,1,0:T(8,128)(2,1)} %param.15) | copy-start | bytes 3145732
  9.4 16.3 %all-to-all-start = ((bf16[16,8,1024]{2,1,0:T(8,128)(2,1)}), bf16[16,8,1024]{2,1,0:T(8,128)(2,1)S(1)}, u32[]{:S(2)}, u32[]{:S(2)}) async-start(bf16[16,8,1024]{2,1,0:T(8,128)(2,1)} %get-tuple-element.38), calls=%async_computation | async-start | bytes 524288 | tf_op jit(solution)/shard_map/all_to_all | solution.py:232
  121.1 15.5 %copy-start.29 = (f32[1,1024]{1,0:T(1,128)S(1)}, f32[1,1024]{1,0:T(1,128)}, u32[]{:S(2)}) copy-start(f32[1,1024]{1,0:T(1,128)} %get-tuple-element.43.refs_7_) | copy-start | bytes 12292
  121.1 15.5 %copy-start.30 = (f32[1,1024]{1,0:T(1,128)S(1)}, f32[1,1024]{1,0:T(1,128)}, u32[]{:S(2)}) copy-start(f32[1,1024]{1,0:T(1,128)} %get-tuple-element.44.refs_8_) | copy-start | bytes 12292
  121.2 15.5 %copy-start.31 = (f32[1,1024]{1,0:T(1,128)S(1)}, f32[1,1024]{1,0:T(1,128)}, u32[]{:S(2)}) copy-start(f32[1,1024]{1,0:T(1,128)} %get-tuple-element.45.refs_9_) | copy-start | bytes 12292
  139.9 15.9 %copy-start.24 = (bf16[64,512]{1,0:T(8,128)(2,1)S(1)}, bf16[64,512]{1,0:T(8,128)(2,1)}, u32[]{:S(2)}) copy-start(bf16[64,512]{1,0:T(8,128)(2,1)} %get-tuple-element.58.refs_8_) | copy-start | bytes 196612
  140.0 15.9 %copy-start.26 = (bf16[64,512]{1,0:T(8,128)(2,1)S(1)}, bf16[64,512]{1,0:T(8,128)(2,1)}, u32[]{:S(2)}) copy-start(bf16[64,512]{1,0:T(8,128)(2,1)} %get-tuple-element.59.refs_9_) | copy-start | bytes 196612
  151.5 4.4 %copy-start.15 = (bf16[64,1024]{1,0:T(8,128)(2,1)S(1)}, bf16[64,1024]{1,0:T(8,128)(2,1)}, u32[]{:S(2)}) copy-start(bf16[64,1024]{1,0:T(8,128)(2,1)} %get-tuple-element.54.refs_4_) | copy-start | bytes 393220
  151.5 4.4 %copy-start.18 = (bf16[64,512]{1,0:T(8,128)(2,1)S(1)}, bf16[64,512]{1,0:T(8,128)(2,1)}, u32[]{:S(2)}) copy-start(bf16[64,512]{1,0:T(8,128)(2,1)} %get-tuple-element.55.refs_5_) | copy-start | bytes 196612
  151.5 4.4 %copy-start.21 = (bf16[64,512]{1,0:T(8,128)(2,1)S(1)}, bf16[64,512]{1,0:T(8,128)(2,1)}, u32[]{:S(2)}) copy-start(bf16[64,512]{1,0:T(8,128)(2,1)} %get-tuple-element.56.refs_6_) | copy-start | bytes 196612
  151.5 4.4 %copy-start.23 = (bf16[64,512]{1,0:T(8,128)(2,1)S(1)}, bf16[64,512]{1,0:T(8,128)(2,1)}, u32[]{:S(2)}) copy-start(bf16[64,512]{1,0:T(8,128)(2,1)} %get-tuple-element.57.refs_7_) | copy-start | bytes 196612
  152.2 3.7 %copy-start.7 = (bf16[64,1024]{1,0:T(8,128)(2,1)S(1)}, bf16[64,1024]{1,0:T(8,128)(2,1)}, u32[]{:S(2)}) copy-start(bf16[64,1024]{1,0:T(8,128)(2,1)} %get-tuple-element.50.refs_0_) | copy-start | bytes 393220
  152.2 3.7 %copy-start.10 = (bf16[64,1024]{1,0:T(8,128)(2,1)S(1)}, bf16[64,1024]{1,0:T(8,128)(2,1)}, u32[]{:S(2)}) copy-start(bf16[64,1024]{1,0:T(8,128)(2,1)} %get-tuple-element.51.refs_1_) | copy-start | bytes 393220
  152.2 3.7 %copy-start.12 = (bf16[64,1024]{1,0:T(8,128)(2,1)S(1)}, bf16[64,1024]{1,0:T(8,128)(2,1)}, u32[]{:S(2)}) copy-start(bf16[64,1024]{1,0:T(8,128)(2,1)} %get-tuple-element.52.refs_2_) | copy-start | bytes 393220
  152.2 3.7 %copy-start.13 = (bf16[64,1024]{1,0:T(8,128)(2,1)S(1)}, bf16[64,1024]{1,0:T(8,128)(2,1)}, u32[]{:S(2)}) copy-start(bf16[64,1024]{1,0:T(8,128)(2,1)} %get-tuple-element.53.refs_3_) | copy-start | bytes 393220
  152.2 11.4 %all-to-all-start.9 = ((bf16[16,8,1024]{2,1,0:T(8,128)(2,1)}), bf16[16,8,1024]{2,1,0:T(8,128)(2,1)S(1)}, u32[]{:S(2)}, u32[]{:S(2)}) async-start(bf16[16,8,1024]{2,1,0:T(8,128)(2,1)} %get-tuple-element.47), calls=%async_computation.9 | async-start | bytes 524288 | tf_op jit(solution)/shard_map/all_to_all | solution.py:232
  156.0 1.8 %copy-start.6 = (bf16[64,1024]{1,0:T(8,128)(2,1)S(1)}, bf16[64,1024]{1,0:T(8,128)(2,1)}, u32[]{:S(2)}) copy-start(bf16[64,1024]{1,0:T(8,128)(2,1)} %get-tuple-element.65.refs_5_) | copy-start | bytes 393220
  156.0 1.8 %copy-start.8 = (bf16[64,1024]{1,0:T(8,128)(2,1)S(1)}, bf16[64,1024]{1,0:T(8,128)(2,1)}, u32[]{:S(2)}) copy-start(bf16[64,1024]{1,0:T(8,128)(2,1)} %get-tuple-element.66.refs_6_) | copy-start | bytes 393220
  156.0 1.8 %copy-start.9 = (bf16[64,1024]{1,0:T(8,128)(2,1)S(1)}, bf16[64,1024]{1,0:T(8,128)(2,1)}, u32[]{:S(2)}) copy-start(bf16[64,1024]{1,0:T(8,128)(2,1)} %get-tuple-element.67.refs_7_) | copy-start | bytes 393220
  156.0 1.8 %copy-start.11 = (bf16[64,1024]{1,0:T(8,128)(2,1)S(1)}, bf16[64,1024]{1,0:T(8,128)(2,1)}, u32[]{:S(2)}) copy-start(bf16[64,1024]{1,0:T(8,128)(2,1)} %get-tuple-element.68.refs_8_) | copy-start | bytes 393220
  156.0 1.8 %copy-start.14 = (bf16[64,1024]{1,0:T(8,128)(2,1)S(1)}, bf16[64,1024]{1,0:T(8,128)(2,1)}, u32[]{:S(2)}) copy-start(bf16[64,1024]{1,0:T(8,128)(2,1)} %get-tuple-element.69.refs_9_) | copy-start | bytes 393220
  156.0 1.8 %copy-start.17 = (bf16[64,512]{1,0:T(8,128)(2,1)S(1)}, bf16[64,512]{1,0:T(8,128)(2,1)}, u32[]{:S(2)}) copy-start(bf16[64,512]{1,0:T(8,128)(2,1)} %get-tuple-element.60.refs_0_) | copy-start | bytes 196612
  156.0 1.8 %copy-start.19 = (bf16[64,512]{1,0:T(8,128)(2,1)S(1)}, bf16[64,512]{1,0:T(8,128)(2,1)}, u32[]{:S(2)}) copy-start(bf16[64,512]{1,0:T(8,128)(2,1)} %get-tuple-element.61.refs_1_) | copy-start | bytes 196612
  (10 other events, 11.7 us)

commit v3 on v2

--- a/solution.py
+++ b/solution.py
@@ -83,34 +83,49 @@
 def step_kernel(peers, step, last, *refs):
     refs = list(refs)
     take = lambda count: [refs.pop(0) for _ in range(count)]
-    plan, stashed = take(2)
-    sources = take(1 if step else 2)
-    gain_ref, weight_in, weight_out = take(3)
-    gains = take(step if last else 0)
+    first = step == 0
+    operands = take(9 if first else 6 + (step if last else 0))
     (parts_out,) = take(1)
     targets = take(4 if last else 5)
+    feeds_out = take(2 if first else 0)
     slot_ref, *kept = take(6)
-    gains_kept = take(len(gains))
-    (sems,) = take(1)
-
-    fetches = [pltpu.make_async_copy(stashed.at[plan[0, step]], slot_ref, sems.at[0])]
-    fetches += [
-        pltpu.make_async_copy(ref, target, sems.at[6 + k]) for k, (ref, target) in enumerate(zip(gains, gains_kept))
-    ]
-    for fetch in fetches:
-        fetch.start()
-    stores = [pltpu.make_async_copy(ref, target, sems.at[1 + k]) for k, (ref, target) in enumerate(zip(kept, targets))]
+    *held, sems = refs
+    count = iter(range(sems.shape[0]))
+
+    def copy(source, target):
+        return pltpu.make_async_copy(source, target, sems.at[next(count)])
+
+    def begin(sources, targets):
+        copies = [copy(source, target) for source, target in zip(sources, targets)]
+        for one in copies:
+            one.start()
+        return copies
+
+    if first:
+        plan_hbm, stashed, rows_hbm, grads_hbm, *more = operands
+        plan, rows_ref, grads_ref, gain_ref, weight_in, weight_out = held
+        (planned,) = begin([plan_hbm], [plan])
+        fetches = begin([grads_hbm, more[2], more[0], rows_hbm, more[1]], [grads_ref, weight_out, gain_ref, rows_ref, weight_in])
+        own = pl.multiple_of(lax.axis_index("mp") * feeds_out[0].shape[1], feeds_out[0].shape[1])
+        feed_copies = begin([feed.at[:, pl.ds(own, feeds_out[0].shape[1]), :] for feed in more[3:]], feeds_out)
+        planned.wait()
+        (slot_copy,) = begin([stashed.at[plan[0, step]]], [slot_ref])
+        for fetch in fetches:
+            fetch.wait()
+        inputs, grads_low = rows_ref[...].astype(F32), grads_ref[...]
+        grads = grads_low.astype(F32)
+    else:
+        plan, stashed, received, gain_ref, weight_in, weight_out, *gains = operands
+        (slot_copy,) = begin([stashed.at[plan[0, step]]], [slot_ref])
+        gain_copies = begin(gains, held)
+        inputs, grads = flat(received, peers, 0), flat(received, peers, peers)
+        grads_low = grads.astype(BF16)
+    stores = [copy(ref, target) for ref, target in zip(kept, targets)]
 
     def keep(which, value):
         kept[which][...] = value
         stores[which].start()
 
-    if step:
-        inputs, grads = flat(sources[0], peers, 0), flat(sources[0], peers, peers)
-        grads_low = grads.astype(BF16)
-    else:
-        inputs, grads_low = sources[0][...].astype(F32), sources[1][...]
-        grads = grads_low.astype(F32)
     keep(2, grads_low)
     gain = gain_ref[...].astype(F32)
     portion = 1.0 / peers
@@ -119,13 +134,10 @@
     hidden_grad = against_rows(grads_low, weight_out[...])
     _, inverse, projected = normalize(inputs, gain, weight_in[...])
 
-    fetches[0].wait()
+    slot_copy.wait()
     slot = slot_ref[...].astype(F32)
     slot_scaled, slot_inverse, slot_projected = normalize(slot, gain, weight_in[...])
     keep(1, slot_scaled)
-
-    hidden = gelu_parts(inverse * projected)[0].astype(BF16)
-    forward = times(hidden, weight_out[...]) + inputs * portion
 
     slot_preact = slot_inverse * slot_projected
     slot_hidden, *about = gelu_parts(slot_preact)
@@ -137,14 +149,18 @@
     inner = jnp.sum(pre_grad * slot_projected, axis=1, keepdims=True)
     factor = inner * slot_inverse * slot_inverse * slot_inverse * (-1.0 / D)
     gain_sum = jnp.sum(input_part * slot, axis=0, keepdims=True)
+    if not last:
+        keep(4, gain_sum)
     backward = grads * portion + input_part * gain + factor * slot
-
+    backward = backward.reshape(peers, share, D).astype(BF16)
+
+    hidden = gelu_parts(inverse * projected)[0].astype(BF16)
+    forward = times(hidden, weight_out[...]) + inputs * portion
     forward = forward.reshape(peers, share, D).astype(BF16)
-    backward = backward.reshape(peers, share, D).astype(BF16)
     if last:
         parts_out[:peers, :, :D] = forward
         parts_out[peers:, :, :D] = backward
-        for fetch, ref in zip(fetches[1:], gains_kept):
+        for fetch, ref in zip(gain_copies, held):
             fetch.wait()
             gain_sum = gain_sum + ref[...]
         stack = jnp.concatenate([gain_sum[:, k * LANES : (k + 1) * LANES] for k in range(D // LANES)], axis=0)
@@ -154,11 +170,13 @@
             parts_out[k, :, D : D + LANES] = high
             parts_out[k, :, D + LANES :] = low
     else:
-        keep(4, gain_sum)
         parts_out[:peers] = backward
         parts_out[peers:] = forward
     for store in stores:
         store.wait()
+    if first:
+        for fetch in feed_copies:
+            fetch.wait()
 
 
 def sum_kernel(peers, sections, step, received, feed_rows, feed_grads, spread_out):
@@ -217,16 +235,13 @@
     peers = lax.axis_size("mp")
     even_pairs = pair_groups(sections, peers, 0)
     odd_pairs = pair_groups(sections, peers, 1)
-    weight_in = in_vmem(enter_weight[0])
-    weight_out = in_vmem(leave_weight[0])
-    gain = in_vmem(norm_gain)
-    stashed = pltpu.with_memory_space_constraint(stashed_rows[0], pltpu.HBM)
+    in_hbm = lambda value: pltpu.with_memory_space_constraint(value, pltpu.HBM)
+    weights = (enter_weight[0], leave_weight[0])
+    stashed = in_hbm(stashed_rows[0])
     steps, rows = stashed.shape[0], stashed.shape[1]
     width = enter_weight.shape[2]
     share = rows // peers
     matmul = 2 * rows * D * width
-    own = lax.axis_index("mp") * share
-    feeds = [in_vmem(lax.dynamic_slice_in_dim(feed, own, share, 1)) for feed in (feed_rows, feed_grads)]
 
     def exchange(parts, groups):
         return in_vmem(lax.all_to_all(parts, BOTH, 0, 0, axis_index_groups=groups, tiled=True))
@@ -236,32 +251,42 @@
         return call(kernel, outs, args, 1 << 18)
 
     kept = [((rows, width), BF16), ((rows, D), BF16), ((rows, D), BF16), ((rows, width), BF16), ((1, D), F32)]
-    source = (in_vmem(arrive_rows[0]), in_vmem(arrive_grads[0]))
     stored = [[] for _ in kept]
     for step in range(steps):
-        last = step + 1 == steps
-        gains = stored[4] if last else []
-        args = [slot_order, stashed, *source, gain, weight_in, weight_out, *gains]
+        first, last = step == 0, step + 1 == steps
         outs = [((2 * peers, share, D + 2 * LANES if last else D), BF16, "vmem")]
         outs += [(shape, dtype, "hbm") for shape, dtype in kept[: 4 if last else 5]]
-        scratch = [pltpu.VMEM((rows, D), BF16), *(pltpu.VMEM(*k) for k in kept), *(pltpu.VMEM((1, D), F32) for _ in gains)]
-        scratch.append(pltpu.SemaphoreType.DMA((6 + steps,)))
+        scratch = [pltpu.VMEM((rows, D), BF16), *(pltpu.VMEM(*k) for k in kept)]
+        if first:
+            args = [slot_order, stashed, arrive_rows[0], arrive_grads[0], norm_gain, *weights, feed_rows, feed_grads]
+            args = [in_hbm(arg) for arg in args]
+            places = {"hbm": range(len(args))}
+            outs += [((steps - 1, share, D), BF16, "vmem")] * 2
+            scratch += [pltpu.SMEM(slot_order.shape, jnp.int32)]
+            scratch += [pltpu.VMEM(arg.shape, BF16) for arg in args[2:7]]
+        else:
+            gains = [in_hbm(part) for part in stored[4]] if last else []
+            args = [slot_order, stashed, source, in_vmem(norm_gain), *map(in_vmem, weights), *gains]
+            places = {"smem": (0,), "hbm": (1, *range(6, len(args)))}
+            scratch += [pltpu.VMEM((1, D), F32) for _ in gains]
+        scratch.append(pltpu.SemaphoreType.DMA((16,)))
         kernel = lambda *refs: step_kernel(peers, step, last, *refs)
-        in_hbm = [1, *range(len(args) - len(gains), len(args))]
-        parts, *results = call(kernel, outs, args, 5 * matmul, smem=(0,), hbm=in_hbm, scratch=scratch)
+        parts, *results = call(kernel, outs, args, 5 * matmul, scratch=scratch, **places)
+        if first:
+            *results, feed_inputs, feed_losses = results
         for past, result in zip(stored, results):
             past.append(result)
         if last:
             break
-        (parts,) = spread(
-            lambda *refs: sum_kernel(peers, sections, step, *refs), [], exchange(parts, odd_pairs), *feeds
-        )
-        source = (exchange(parts, even_pairs),)
+        kernel = lambda *refs: sum_kernel(peers, sections, step, *refs)
+        (parts,) = spread(kernel, [], exchange(parts, odd_pairs), feed_inputs, feed_losses)
+        source = exchange(parts, even_pairs)
+    received = exchange(parts, even_pairs)
 
     parts, gain_total = spread(
         lambda *refs: last_sum_kernel(peers, *refs),
         [((D // LANES, LANES), F32, "any")],
-        exchange(parts, even_pairs),
+        received,
     )
     received = exchange(parts, even_pairs)
     kernel = lambda *refs: finish_kernel(peers, *refs)

time: 165 us -> 159 us (0.964)
  blocking collectives: 113 us -> 129 us
  starting transfers between devices: 12.1 us -> 3.63 us
  waiting for transfers between devices: 11 us -> 4.05 us
  local copies, waits for them, and re-layouts: 6.6 us -> 0.11 us
    all_to_all x8 -> x9, blocking collectives: 113 us -> 129 us  [exchange(): lax.all_to_all(parts, BOTH, 0, 0, axis_index_groups=groups, tiled=True)]
    all_to_all x2 -> x1, starting transfers between devices: 12.1 us -> 3.63 us  [exchange(): lax.all_to_all(parts, BOTH, 0, 0, axis_index_groups=groups, tiled=True)]
    all_to_all x2 -> x1, waiting for transfers between devices: 11 us -> 4.05 us  [exchange(): lax.all_to_all(parts, BOTH, 0, 0, axis_index_groups=groups, tiled=True)]
    unnamed x64 -> x48, local copies, waits for them, and re-layouts: 5.71 us -> 0.11 us
  transfers between devices with their start and end apart: 2 -> 1, of which waited for: 2 -> 1; matrix products, arithmetic and copies ran while one was open for 1% -> 0% of each run, Pallas kernels for 2% -> 2%
where the time goes in v3:
time: 159 us
  blocking collectives  129 us (81%)
  Pallas kernels  20.7 us (13%)
  waiting for transfers between devices  4.05 us (3%)
  starting transfers between devices  3.63 us (2%)
    all_to_all x9, blocking collectives, exchange(): lax.all_to_all(parts, BOTH, 0, 0, axis_index_groups=groups, tiled=True)  129 us
    pallas_call x13, Pallas kernels, call(): pl.pallas_call(kernel, out_shape=[{'vmem': pltpu.VMEM, 'hbm': pltpu.HBM,...  20.7 us
    all_to_all x1, waiting for transfers between devices, exchange(): lax.all_to_all(parts, BOTH, 0, 0, axis_index_groups=groups, tiled=True)  4.05 us
    all_to_all x1, starting transfers between devices, exchange(): lax.all_to_all(parts, BOTH, 0, 0, axis_index_groups=groups, tiled=True)  3.63 us
  transfers between devices with their start and end apart: 1, of which 1 were waited for; matrix products, arithmetic and copies ran while one was open for 0% of the time, Pallas kernels for 2%

profile of v3, /device:TPU:1, one launch (start us, length us, event | category | flops | bytes accessed | tf_op | source)
XLA Modules:
  0.0 158.6 jit_solution(10321136489914316801)
XLA Ops:
  0.6 3.9 %shard_map.128 = (bf16[16,8,1024]{2,1,0:T(8,128)(2,1)S(1)}, bf16[64,512]{1,0:T(8,128)(2,1)}, bf16[64,1024]{1,0:T(8,128)(2,1)}, bf16[64,1024]{1,0:T(8,128)(2,1)},...) custom-call(s32[1,5]{1,0:T(1,128)} %refs_0_.9, ...), custom_call_target="tpu_custom_call" | custom-call | flops 335544320 | bytes 1048576 | tf_op jit(solution)/shard_map/pallas_call | solution.py:45
  4.6 0.0 copy-start
  4.6 16.1 %all_to_all.50.refs_0_ = bf16[16,8,1024]{2,1,0:T(8,128)(2,1)S(1)} all-to-all(bf16[16,8,1024]{2,1,0:T(8,128)(2,1)S(1)} %get-tuple-element.40), channel_id=1, replica_groups={{8,9,10,11,12,13,14,15,16,17,18,19,20,21,22,23},{24,25,26,27,28,29,30,3..., dimensions={0} | all-to-all | bytes 524288 | tf_op jit(solution)/shard_map/all_to_all | solution.py:247
  20.7 0.0 copy-start.12
  20.7 0.0 copy-start.23
  20.7 23.1 %all_to_all.51.refs_2_ = bf16[16,8,1024]{2,1,0:T(8,128)(2,1)S(1)} all-to-all(bf16[16,8,1024]{2,1,0:T(8,128)(2,1)S(1)} %shard_map.129), channel_id=1, replica_groups={{0,1,2,3,4,5,6,7,8,9,10,11,12,13,14,15},{16,17,18,19,20,21,22,23,24,25,..., dimensions={0} | all-to-all | bytes 524288 | tf_op jit(solution)/shard_map/all_to_all | solution.py:247
  43.9 3.0 %shard_map.130 = (bf16[16,8,1024]{2,1,0:T(8,128)(2,1)S(1)}, bf16[64,512]{1,0:T(8,128)(2,1)}, bf16[64,1024]{1,0:T(8,128)(2,1)}, bf16[64,1024]{1,0:T(8,128)(2,1)},...) custom-call(s32[1,5]{1,0:T(1,128)S(1)} %copy-done.23, bf16[5,64,1024]{2,1,0:T(8,128)(2,1)} %bitcast.21, ...), custom_call_target="tpu_custom_call" | custom-call | flops 335544320 | bytes 1048576 | tf_op jit(solution)/shard_map/pallas_call | solution.py:45
  46.9 10.7 %all_to_all.52.refs_0_ = bf16[16,8,1024]{2,1,0:T(8,128)(2,1)S(1)} all-to-all(bf16[16,8,1024]{2,1,0:T(8,128)(2,1)S(1)} %get-tuple-element.43), channel_id=1, replica_groups={{8,9,10,11,12,13,14,15,16,17,18,19,20,21,22,23},{24,25,26,27,28,29,30,3..., dimensions={0} | all-to-all | bytes 524288 | tf_op jit(solution)/shard_map/all_to_all | solution.py:247
  57.7 15.5 %all_to_all.53.refs_2_ = bf16[16,8,1024]{2,1,0:T(8,128)(2,1)S(1)} all-to-all(bf16[16,8,1024]{2,1,0:T(8,128)(2,1)S(1)} %shard_map.131), channel_id=1, replica_groups={{0,1,2,3,4,5,6,7,8,9,10,11,12,13,14,15},{16,17,18,19,20,21,22,23,24,25,..., dimensions={0} | all-to-all | bytes 524288 | tf_op jit(solution)/shard_map/all_to_all | solution.py:247
  73.1 3.0 %shard_map.132 = (bf16[16,8,1024]{2,1,0:T(8,128)(2,1)S(1)}, bf16[64,512]{1,0:T(8,128)(2,1)}, bf16[64,1024]{1,0:T(8,128)(2,1)}, bf16[64,1024]{1,0:T(8,128)(2,1)},...) custom-call(s32[1,5]{1,0:T(1,128)S(1)} %copy-done.23, bf16[5,64,1024]{2,1,0:T(8,128)(2,1)} %bitcast.22, ...), custom_call_target="tpu_custom_call" | custom-call | flops 335544320 | bytes 1048576 | tf_op jit(solution)/shard_map/pallas_call | solution.py:45
  76.2 10.7 %all_to_all.54.refs_0_ = bf16[16,8,1024]{2,1,0:T(8,128)(2,1)S(1)} all-to-all(bf16[16,8,1024]{2,1,0:T(8,128)(2,1)S(1)} %get-tuple-element.44), channel_id=1, replica_groups={{8,9,10,11,12,13,14,15,16,17,18,19,20,21,22,23},{24,25,26,27,28,29,30,3..., dimensions={0} | all-to-all | bytes 524288 | tf_op jit(solution)/shard_map/all_to_all | solution.py:247
  86.9 15.5 %all_to_all.55.refs_2_ = bf16[16,8,1024]{2,1,0:T(8,128)(2,1)S(1)} all-to-all(bf16[16,8,1024]{2,1,0:T(8,128)(2,1)S(1)} %shard_map.133), channel_id=1, replica_groups={{0,1,2,3,4,5,6,7,8,9,10,11,12,13,14,15},{16,17,18,19,20,21,22,23,24,25,..., dimensions={0} | all-to-all | bytes 524288 | tf_op jit(solution)/shard_map/all_to_all | solution.py:247
  102.4 3.0 %shard_map.134 = (bf16[16,8,1024]{2,1,0:T(8,128)(2,1)S(1)}, bf16[64,512]{1,0:T(8,128)(2,1)}, bf16[64,1024]{1,0:T(8,128)(2,1)}, bf16[64,1024]{1,0:T(8,128)(2,1)},...) custom-call(s32[1,5]{1,0:T(1,128)S(1)} %copy-done.23, bf16[5,64,1024]{2,1,0:T(8,128)(2,1)} %bitcast.23, ...), custom_call_target="tpu_custom_call" | custom-call | flops 335544320 | bytes 1048576 | tf_op jit(solution)/shard_map/pallas_call | solution.py:45
  105.4 10.7 %all_to_all.56.refs_0_ = bf16[16,8,1024]{2,1,0:T(8,128)(2,1)S(1)} all-to-all(bf16[16,8,1024]{2,1,0:T(8,128)(2,1)S(1)} %get-tuple-element.45), channel_id=1, replica_groups={{8,9,10,11,12,13,14,15,16,17,18,19,20,21,22,23},{24,25,26,27,28,29,30,3..., dimensions={0} | all-to-all | bytes 524288 | tf_op jit(solution)/shard_map/all_to_all | solution.py:247
  116.1 15.5 %all_to_all.57.refs_2_ = bf16[16,8,1024]{2,1,0:T(8,128)(2,1)S(1)} all-to-all(bf16[16,8,1024]{2,1,0:T(8,128)(2,1)S(1)} %shard_map.135), channel_id=1, replica_groups={{0,1,2,3,4,5,6,7,8,9,10,11,12,13,14,15},{16,17,18,19,20,21,22,23,24,25,..., dimensions={0} | all-to-all | bytes 524288 | tf_op jit(solution)/shard_map/all_to_all | solution.py:247
  131.6 2.6 %shard_map.136 = (bf16[16,8,1280]{2,1,0:T(8,128)(2,1)S(1)}, bf16[64,512]{1,0:T(8,128)(2,1)}, bf16[64,1024]{1,0:T(8,128)(2,1)}, bf16[64,1024]{1,0:T(8,128)(2,1)}, bf16[64,512]{1,0:T(8,128)(2,1)}) custom-call(s32[1,5]{1,0:T(1,128)S(1)} %copy-done.23, bf16[5,64,1024]{2,1,0:T(8,128)(2,1)} %bitcast.24, bf16[16,8,1024]{2,1,0:T(8,128)(2,1)S(1)} %all_to_all.57.refs_2_, ...), custom_call_target="tpu_custom_call" | custom-call | flops 335544320 | bytes 1048576 | tf_op jit(solution)/shard_map/pallas_call | solution.py:45
  134.3 11.5 %all_to_all.58.refs_0_ = bf16[16,8,1280]{2,1,0:T(8,128)(2,1)S(1)} all-to-all(bf16[16,8,1280]{2,1,0:T(8,128)(2,1)S(1)} %get-tuple-element.50), channel_id=1, replica_groups={{0,1,2,3,4,5,6,7,8,9,10,11,12,13,14,15},{16,17,18,19,20,21,22,23,24,25,..., dimensions={0} | all-to-all | bytes 655360 | tf_op jit(solution)/shard_map/all_to_all | solution.py:247
  145.8 0.7 shard_map.137
  146.5 3.6 %all-to-all-start.9 = ((bf16[16,8,1024]{2,1,0:T(8,128)(2,1)}), bf16[16,8,1024]{2,1,0:T(8,128)(2,1)S(1)}, u32[]{:S(2)}, u32[]{:S(2)}) async-start(bf16[16,8,1024]{2,1,0:T(8,128)(2,1)} %get-tuple-element.51), calls=%async_computation.9 | async-start | bytes 524288 | tf_op jit(solution)/shard_map/all_to_all | solution.py:247
  150.3 0.0 copy-start.2
  150.4 1.7 %shard_map.139 = bf16[1024,512]{1,0:T(8,128)(2,1)} custom-call(bf16[64,1024]{1,0:T(8,128)(2,1)S(1)} %copy-done.4, bf16[64,1024]{1,0:T(8,128)(2,1)S(1)} %copy-done.6, bf16[64,1024]{1,0:T(8,128)(2,1)S(1)} %copy-done.8, bf16[64,1024]{1,0:T(8,128)(2,1)S(1)} %copy-done.9, bf16[64,1024]{1,0:T(8,128)(2,1)S(1)} %copy-done.11, bf16[64,512]{1,0:T(8,128)(2,1)S(1)} %copy-done.15, ...), custom_call_target="tpu_custom_call" | custom-call | flops 335544320 | bytes 1048576 | tf_op jit(solution)/shard_map/pallas_call | solution.py:45
  152.1 1.7 %shard_map.140 = bf16[512,1024]{1,0:T(8,128)(2,1)} custom-call(bf16[64,512]{1,0:T(8,128)(2,1)S(1)} %copy-done.13, bf16[64,512]{1,0:T(8,128)(2,1)S(1)} %copy-done.14, bf16[64,512]{1,0:T(8,128)(2,1)S(1)} %copy-done.16, bf16[64,512]{1,0:T(8,128)(2,1)S(1)} %copy-done.18, bf16[64,512]{1,0:T(8,128)(2,1)S(1)} %copy-done.21, bf16[64,1024]{1,0:T(8,128)(2,1)S(1)} %copy-done.2, ...), custom_call_target="tpu_custom_call" | custom-call | flops 335544320 | bytes 1048576 | tf_op jit(solution)/shard_map/pallas_call | solution.py:45
  153.9 4.1 %all-to-all-done.9.refs_0_ = bf16[16,8,1024]{2,1,0:T(8,128)(2,1)S(1)} async-done(((bf16[16,8,1024]{2,1,0:T(8,128)(2,1)}), bf16[16,8,1024]{2,1,0:T(8,128)(2,1)S(1)}, u32[]{:S(2)}, u32[]{:S(2)}) %all-to-all-start.9) | async-done | bytes 262176 | tf_op jit(solution)/shard_map/all_to_all | solution.py:247
  157.9 0.7 shard_map.138
  (48 shorter events, 0.3 us)
Async XLA Ops:
  0.6 43.2 %copy-start.1 = (bf16[1,512,1024]{2,1,0:T(8,128)(2,1)S(1)}, bf16[1,512,1024]{2,1,0:T(8,128)(2,1)}, u32[]{:S(2)}) copy-start(bf16[1,512,1024]{2,1,0:T(8,128)(2,1)} %param.16) | copy-start | bytes 3145732
  4.6 39.3 %copy-start = (bf16[1,1024,512]{2,1,0:T(8,128)(2,1)S(1)}, bf16[1,1024,512]{2,1,0:T(8,128)(2,1)}, u32[]{:S(2)}) copy-start(bf16[1,1024,512]{2,1,0:T(8,128)(2,1)} %param.15) | copy-start | bytes 3145732
  20.7 23.2 %copy-start.12 = (bf16[1,1024]{1,0:T(2,128)(2,1)S(1)}, bf16[1,1024]{1,0:T(2,128)(2,1)}, u32[]{:S(2)}) copy-start(bf16[1,1024]{1,0:T(2,128)(2,1)} %refs_3_.7) | copy-start | bytes 6148
  20.7 23.1 %copy-start.23 = (s32[1,5]{1,0:T(1,128)S(1)}, s32[1,5]{1,0:T(1,128)}, u32[]{:S(2)}) copy-start(s32[1,5]{1,0:T(1,128)} %refs_0_.9) | copy-start | bytes 64
  134.2 15.9 %copy-start.20 = (bf16[64,512]{1,0:T(8,128)(2,1)S(1)}, bf16[64,512]{1,0:T(8,128)(2,1)}, u32[]{:S(2)}) copy-start(bf16[64,512]{1,0:T(8,128)(2,1)} %get-tuple-element.62.refs_8_) | copy-start | bytes 196612
  134.3 15.9 %copy-start.22 = (bf16[64,512]{1,0:T(8,128)(2,1)S(1)}, bf16[64,512]{1,0:T(8,128)(2,1)}, u32[]{:S(2)}) copy-start(bf16[64,512]{1,0:T(8,128)(2,1)} %get-tuple-element.63.refs_9_) | copy-start | bytes 196612
  145.8 4.4 %copy-start.11 = (bf16[64,1024]{1,0:T(8,128)(2,1)S(1)}, bf16[64,1024]{1,0:T(8,128)(2,1)}, u32[]{:S(2)}) copy-start(bf16[64,1024]{1,0:T(8,128)(2,1)} %get-tuple-element.58.refs_4_) | copy-start | bytes 393220
  145.8 4.4 %copy-start.15 = (bf16[64,512]{1,0:T(8,128)(2,1)S(1)}, bf16[64,512]{1,0:T(8,128)(2,1)}, u32[]{:S(2)}) copy-start(bf16[64,512]{1,0:T(8,128)(2,1)} %get-tuple-element.59.refs_5_) | copy-start | bytes 196612
  145.8 4.4 %copy-start.17 = (bf16[64,512]{1,0:T(8,128)(2,1)S(1)}, bf16[64,512]{1,0:T(8,128)(2,1)}, u32[]{:S(2)}) copy-start(bf16[64,512]{1,0:T(8,128)(2,1)} %get-tuple-element.60.refs_6_) | copy-start | bytes 196612
  145.8 4.4 %copy-start.19 = (bf16[64,512]{1,0:T(8,128)(2,1)S(1)}, bf16[64,512]{1,0:T(8,128)(2,1)}, u32[]{:S(2)}) copy-start(bf16[64,512]{1,0:T(8,128)(2,1)} %get-tuple-element.61.refs_7_) | copy-start | bytes 196612
  146.5 3.7 %copy-start.4 = (bf16[64,1024]{1,0:T(8,128)(2,1)S(1)}, bf16[64,1024]{1,0:T(8,128)(2,1)}, u32[]{:S(2)}) copy-start(bf16[64,1024]{1,0:T(8,128)(2,1)} %get-tuple-element.54.refs_0_) | copy-start | bytes 393220
  146.5 3.7 %copy-start.6 = (bf16[64,1024]{1,0:T(8,128)(2,1)S(1)}, bf16[64,1024]{1,0:T(8,128)(2,1)}, u32[]{:S(2)}) copy-start(bf16[64,1024]{1,0:T(8,128)(2,1)} %get-tuple-element.55.refs_1_) | copy-start | bytes 393220
  146.5 3.7 %copy-start.8 = (bf16[64,1024]{1,0:T(8,128)(2,1)S(1)}, bf16[64,1024]{1,0:T(8,128)(2,1)}, u32[]{:S(2)}) copy-start(bf16[64,1024]{1,0:T(8,128)(2,1)} %get-tuple-element.56.refs_2_) | copy-start | bytes 393220
  146.5 3.7 %copy-start.9 = (bf16[64,1024]{1,0:T(8,128)(2,1)S(1)}, bf16[64,1024]{1,0:T(8,128)(2,1)}, u32[]{:S(2)}) copy-start(bf16[64,1024]{1,0:T(8,128)(2,1)} %get-tuple-element.57.refs_3_) | copy-start | bytes 393220
  146.5 11.4 %all-to-all-start.9 = ((bf16[16,8,1024]{2,1,0:T(8,128)(2,1)}), bf16[16,8,1024]{2,1,0:T(8,128)(2,1)S(1)}, u32[]{:S(2)}, u32[]{:S(2)}) async-start(bf16[16,8,1024]{2,1,0:T(8,128)(2,1)} %get-tuple-element.51), calls=%async_computation.9 | async-start | bytes 524288 | tf_op jit(solution)/shard_map/all_to_all | solution.py:247
  150.3 1.8 %copy-start.2 = (bf16[64,1024]{1,0:T(8,128)(2,1)S(1)}, bf16[64,1024]{1,0:T(8,128)(2,1)}, u32[]{:S(2)}) copy-start(bf16[64,1024]{1,0:T(8,128)(2,1)} %get-tuple-element.69.refs_5_) | copy-start | bytes 393220
  150.3 1.8 %copy-start.3 = (bf16[64,1024]{1,0:T(8,128)(2,1)S(1)}, bf16[64,1024]{1,0:T(8,128)(2,1)}, u32[]{:S(2)}) copy-start(bf16[64,1024]{1,0:T(8,128)(2,1)} %get-tuple-element.70.refs_6_) | copy-start | bytes 393220
  150.3 1.8 %copy-start.5 = (bf16[64,1024]{1,0:T(8,128)(2,1)S(1)}, bf16[64,1024]{1,0:T(8,128)(2,1)}, u32[]{:S(2)}) copy-start(bf16[64,1024]{1,0:T(8,128)(2,1)} %get-tuple-element.71.refs_7_) | copy-start | bytes 393220
  150.3 1.8 %copy-start.7 = (bf16[64,1024]{1,0:T(8,128)(2,1)S(1)}, bf16[64,1024]{1,0:T(8,128)(2,1)}, u32[]{:S(2)}) copy-start(bf16[64,1024]{1,0:T(8,128)(2,1)} %get-tuple-element.72.refs_8_) | copy-start | bytes 393220
  150.3 1.8 %copy-start.10 = (bf16[64,1024]{1,0:T(8,128)(2,1)S(1)}, bf16[64,1024]{1,0:T(8,128)(2,1)}, u32[]{:S(2)}) copy-start(bf16[64,1024]{1,0:T(8,128)(2,1)} %get-tuple-element.73.refs_9_) | copy-start | bytes 393220
  150.3 1.8 %copy-start.13 = (bf16[64,512]{1,0:T(8,128)(2,1)S(1)}, bf16[64,512]{1,0:T(8,128)(2,1)}, u32[]{:S(2)}) copy-start(bf16[64,512]{1,0:T(8,128)(2,1)} %get-tuple-element.64.refs_0_) | copy-start | bytes 196612
  150.3 1.8 %copy-start.14 = (bf16[64,512]{1,0:T(8,128)(2,1)S(1)}, bf16[64,512]{1,0:T(8,128)(2,1)}, u32[]{:S(2)}) copy-start(bf16[64,512]{1,0:T(8,128)(2,1)} %get-tuple-element.65.refs_1_) | copy-start | bytes 196612
  150.3 1.8 %copy-start.16 = (bf16[64,512]{1,0:T(8,128)(2,1)S(1)}, bf16[64,512]{1,0:T(8,128)(2,1)}, u32[]{:S(2)}) copy-start(bf16[64,512]{1,0:T(8,128)(2,1)} %get-tuple-element.66.refs_2_) | copy-start | bytes 196612
  150.3 1.8 %copy-start.18 = (bf16[64,512]{1,0:T(8,128)(2,1)S(1)}, bf16[64,512]{1,0:T(8,128)(2,1)}, u32[]{:S(2)}) copy-start(bf16[64,512]{1,0:T(8,128)(2,1)} %get-tuple-element.67.refs_3_) | copy-start | bytes 196612
  (1 other events, 1.8 us)

commit v4 on v3

--- a/solution.py
+++ b/solution.py
@@ -80,103 +80,101 @@
     return part.reshape(part.shape[0] * part.shape[1], part.shape[2])
 
 
-def step_kernel(peers, step, last, *refs):
-    refs = list(refs)
-    take = lambda count: [refs.pop(0) for _ in range(count)]
-    first = step == 0
-    operands = take(9 if first else 6 + (step if last else 0))
-    (parts_out,) = take(1)
-    targets = take(4 if last else 5)
-    feeds_out = take(2 if first else 0)
-    slot_ref, *kept = take(6)
-    *held, sems = refs
+def first_kernel(peers, *refs):
+    plan_hbm, stashed, rows_hbm, grads_hbm, gain_hbm, weight_in_hbm, weight_out_hbm, *feeds = refs[:9]
+    parts_out, *kept = refs[9:15]
+    feeds_out = refs[15:17]
+    later = refs[17:-8]
+    plan, rows_ref, grads_ref, gain_ref, weight_in, weight_out, slot_ref, sems = refs[-8:]
     count = iter(range(sems.shape[0]))
 
-    def copy(source, target):
-        return pltpu.make_async_copy(source, target, sems.at[next(count)])
-
-    def begin(sources, targets):
-        copies = [copy(source, target) for source, target in zip(sources, targets)]
-        for one in copies:
-            one.start()
-        return copies
-
-    if first:
-        plan_hbm, stashed, rows_hbm, grads_hbm, *more = operands
-        plan, rows_ref, grads_ref, gain_ref, weight_in, weight_out = held
-        (planned,) = begin([plan_hbm], [plan])
-        fetches = begin([grads_hbm, more[2], more[0], rows_hbm, more[1]], [grads_ref, weight_out, gain_ref, rows_ref, weight_in])
-        own = pl.multiple_of(lax.axis_index("mp") * feeds_out[0].shape[1], feeds_out[0].shape[1])
-        feed_copies = begin([feed.at[:, pl.ds(own, feeds_out[0].shape[1]), :] for feed in more[3:]], feeds_out)
-        planned.wait()
-        (slot_copy,) = begin([stashed.at[plan[0, step]]], [slot_ref])
-        for fetch in fetches:
-            fetch.wait()
-        inputs, grads_low = rows_ref[...].astype(F32), grads_ref[...]
-        grads = grads_low.astype(F32)
-    else:
-        plan, stashed, received, gain_ref, weight_in, weight_out, *gains = operands
-        (slot_copy,) = begin([stashed.at[plan[0, step]]], [slot_ref])
-        gain_copies = begin(gains, held)
-        inputs, grads = flat(received, peers, 0), flat(received, peers, peers)
-        grads_low = grads.astype(BF16)
-    stores = [copy(ref, target) for ref, target in zip(kept, targets)]
-
-    def keep(which, value):
-        kept[which][...] = value
-        stores[which].start()
-
-    keep(2, grads_low)
+    def begin(source, target):
+        copy = pltpu.make_async_copy(source, target, sems.at[next(count)])
+        copy.start()
+        return copy
+
+    planned = begin(plan_hbm, plan)
+    fetches = [
+        begin(grads_hbm, grads_ref),
+        begin(weight_out_hbm, weight_out),
+        begin(gain_hbm, gain_ref),
+        begin(rows_hbm, rows_ref),
+        begin(weight_in_hbm, weight_in),
+    ]
+    share = feeds_out[0].shape[1]
+    own = pl.multiple_of(lax.axis_index("mp") * share, share)
+    others = [begin(feed.at[:, pl.ds(own, share), :], target) for feed, target in zip(feeds, feeds_out)]
+    planned.wait()
+    fetches.append(begin(stashed.at[plan[0, 0]], slot_ref))
+    others += [begin(stashed.at[plan[0, 1 + k]], target) for k, target in enumerate(later)]
+    for fetch in fetches:
+        fetch.wait()
+    inputs, grads_low = rows_ref[...].astype(F32), grads_ref[...]
+    results = both_ways(peers, inputs, grads_low.astype(F32), grads_low, slot_ref, gain_ref, weight_in, weight_out, kept)
+    place(peers, parts_out, *results[:2])
+    kept[4][...] = results[2]
+    for other in others:
+        other.wait()
+
+
+def later_kernel(peers, last, *refs):
+    received, slot_ref, gain_ref, weight_in, weight_out, *gains = refs[: -5 if last else -6]
+    parts_out, *kept = refs[-5 if last else -6 :]
+    inputs, grads = flat(received, peers, 0), flat(received, peers, peers)
+    forward, backward, gain_sum = both_ways(
+        peers, inputs, grads, grads.astype(BF16), slot_ref, gain_ref, weight_in, weight_out, kept
+    )
+    if not last:
+        place(peers, parts_out, forward, backward)
+        kept[4][...] = gain_sum
+        return
+    parts_out[:peers, :, :D] = forward
+    parts_out[peers:, :, :D] = backward
+    for ref in gains:
+        gain_sum = gain_sum + ref[...]
+    stack = jnp.concatenate([gain_sum[:, k * LANES : (k + 1) * LANES] for k in range(D // LANES)], axis=0)
+    high = stack.astype(BF16)
+    low = (stack - high.astype(F32)).astype(BF16)
+    for k in range(2 * peers):
+        parts_out[k, :, D : D + LANES] = high
+        parts_out[k, :, D + LANES :] = low
+
+
+def place(peers, parts_out, forward, backward):
+    parts_out[:peers] = backward
+    parts_out[peers:] = forward
+
+
+def both_ways(peers, inputs, grads, grads_low, slot_ref, gain_ref, weight_in, weight_out, kept):
+    hidden_out, scaled_out, grads_out, update_out = kept[:4]
+    grads_out[...] = grads_low
     gain = gain_ref[...].astype(F32)
     portion = 1.0 / peers
     share = inputs.shape[0] // peers
 
     hidden_grad = against_rows(grads_low, weight_out[...])
     _, inverse, projected = normalize(inputs, gain, weight_in[...])
-
-    slot_copy.wait()
     slot = slot_ref[...].astype(F32)
     slot_scaled, slot_inverse, slot_projected = normalize(slot, gain, weight_in[...])
-    keep(1, slot_scaled)
+    scaled_out[...] = slot_scaled
 
     slot_preact = slot_inverse * slot_projected
     slot_hidden, *about = gelu_parts(slot_preact)
-    keep(0, slot_hidden.astype(BF16))
+    hidden_out[...] = slot_hidden.astype(BF16)
     pre_grad = hidden_grad * gelu_slope(slot_preact, *about)
     update = (slot_inverse * pre_grad).astype(BF16)
-    keep(3, update)
+    update_out[...] = update
     input_part = against_rows(update, weight_in[...])
     inner = jnp.sum(pre_grad * slot_projected, axis=1, keepdims=True)
     factor = inner * slot_inverse * slot_inverse * slot_inverse * (-1.0 / D)
     gain_sum = jnp.sum(input_part * slot, axis=0, keepdims=True)
-    if not last:
-        keep(4, gain_sum)
     backward = grads * portion + input_part * gain + factor * slot
     backward = backward.reshape(peers, share, D).astype(BF16)
 
     hidden = gelu_parts(inverse * projected)[0].astype(BF16)
     forward = times(hidden, weight_out[...]) + inputs * portion
     forward = forward.reshape(peers, share, D).astype(BF16)
-    if last:
-        parts_out[:peers, :, :D] = forward
-        parts_out[peers:, :, :D] = backward
-        for fetch, ref in zip(gain_copies, held):
-            fetch.wait()
-            gain_sum = gain_sum + ref[...]
-        stack = jnp.concatenate([gain_sum[:, k * LANES : (k + 1) * LANES] for k in range(D // LANES)], axis=0)
-        high = stack.astype(BF16)
-        low = (stack - high.astype(F32)).astype(BF16)
-        for k in range(2 * peers):
-            parts_out[k, :, D : D + LANES] = high
-            parts_out[k, :, D + LANES :] = low
-    else:
-        parts_out[:peers] = backward
-        parts_out[peers:] = forward
-    for store in stores:
-        store.wait()
-    if first:
-        for fetch in feed_copies:
-            fetch.wait()
+    return forward, backward, gain_sum
 
 
 def sum_kernel(peers, sections, step, received, feed_rows, feed_grads, spread_out):
@@ -253,33 +251,31 @@
     kept = [((rows, width), BF16), ((rows, D), BF16), ((rows, D), BF16), ((rows, width), BF16), ((1, D), F32)]
     stored = [[] for _ in kept]
     for step in range(steps):
-        first, last = step == 0, step + 1 == steps
+        last = step + 1 == steps
         outs = [((2 * peers, share, D + 2 * LANES if last else D), BF16, "vmem")]
-        outs += [(shape, dtype, "hbm") for shape, dtype in kept[: 4 if last else 5]]
-        scratch = [pltpu.VMEM((rows, D), BF16), *(pltpu.VMEM(*k) for k in kept)]
-        if first:
+        outs += [(shape, dtype, "vmem") for shape, dtype in kept[: 4 if last else 5]]
+        if step == 0:
             args = [slot_order, stashed, arrive_rows[0], arrive_grads[0], norm_gain, *weights, feed_rows, feed_grads]
             args = [in_hbm(arg) for arg in args]
-            places = {"hbm": range(len(args))}
             outs += [((steps - 1, share, D), BF16, "vmem")] * 2
-            scratch += [pltpu.SMEM(slot_order.shape, jnp.int32)]
+            outs += [((rows, D), BF16, "vmem")] * (steps - 1)
+            scratch = [pltpu.SMEM(slot_order.shape, jnp.int32)]
             scratch += [pltpu.VMEM(arg.shape, BF16) for arg in args[2:7]]
+            scratch += [pltpu.VMEM((rows, D), BF16), pltpu.SemaphoreType.DMA((8 + steps,))]
+            kernel = lambda *refs: first_kernel(peers, *refs)
+            parts, *results = call(kernel, outs, args, 5 * matmul, hbm=range(len(args)), scratch=scratch)
+            feeds, later = results[5:7], results[7:]
         else:
-            gains = [in_hbm(part) for part in stored[4]] if last else []
-            args = [slot_order, stashed, source, in_vmem(norm_gain), *map(in_vmem, weights), *gains]
-            places = {"smem": (0,), "hbm": (1, *range(6, len(args)))}
-            scratch += [pltpu.VMEM((1, D), F32) for _ in gains]
-        scratch.append(pltpu.SemaphoreType.DMA((16,)))
-        kernel = lambda *refs: step_kernel(peers, step, last, *refs)
-        parts, *results = call(kernel, outs, args, 5 * matmul, scratch=scratch, **places)
-        if first:
-            *results, feed_inputs, feed_losses = results
+            args = [source, later[step - 1], in_vmem(norm_gain), *map(in_vmem, weights)]
+            args += stored[4] if last else []
+            kernel = lambda *refs: later_kernel(peers, last, *refs)
+            parts, *results = call(kernel, outs, args, 5 * matmul)
         for past, result in zip(stored, results):
             past.append(result)
         if last:
             break
         kernel = lambda *refs: sum_kernel(peers, sections, step, *refs)
-        (parts,) = spread(kernel, [], exchange(parts, odd_pairs), feed_inputs, feed_losses)
+        (parts,) = spread(kernel, [], exchange(parts, odd_pairs), *feeds)
         source = exchange(parts, even_pairs)
     received = exchange(parts, even_pairs)
 

time: 159 us -> 153 us (0.962)
  Pallas kernels: 20.7 us -> 14.6 us
    pallas_call x13, Pallas kernels: 20.7 us -> 14.6 us  [call(): pl.pallas_call(kernel, out_shape=[{'vmem': pltpu.VMEM, 'hbm': pltpu.HBM,...]
where the time goes in v4:
time: 153 us; the launch traced here: 152 us
  blocking collectives  129 us (84%)
  Pallas kernels  14.6 us (10%)
  waiting for transfers between devices  4.33 us (3%)
  starting transfers between devices  3.49 us (2%)
    all_to_all x9, blocking collectives, exchange(): lax.all_to_all(parts, BOTH, 0, 0, axis_index_groups=groups, tiled=True)  129 us
    pallas_call x13, Pallas kernels, call(): pl.pallas_call(kernel, out_shape=[{'vmem': pltpu.VMEM, 'hbm': pltpu.HBM,...  14.6 us
    all_to_all x1, waiting for transfers between devices, exchange(): lax.all_to_all(parts, BOTH, 0, 0, axis_index_groups=groups, tiled=True)  4.33 us
    all_to_all x1, starting transfers between devices, exchange(): lax.all_to_all(parts, BOTH, 0, 0, axis_index_groups=groups, tiled=True)  3.49 us
  transfers between devices with their start and end apart: 1, of which 1 were waited for; matrix products, arithmetic and copies ran while one was open for 0% of the time, Pallas kernels for 2%

profile of v4, /device:TPU:1, one launch (start us, length us, event | category | flops | bytes accessed | tf_op | source)
XLA Modules:
  0.0 152.1 jit_solution(9863748781982877554)
XLA Ops:
  0.6 0.0 copy-start.1
  0.6 3.5 %shard_map.128 = (bf16[16,8,1024]{2,1,0:T(8,128)(2,1)S(1)}, bf16[64,512]{1,0:T(8,128)(2,1)S(1)}, bf16[64,1024]{1,0:T(8,128)(2,1)S(1)}, bf16[64,1024]{1,0:T(8,128...) custom-call(s32[1,5]{1,0:T(1,128)} %refs_0_.1, ...), custom_call_target="tpu_custom_call" | custom-call | flops 335544320 | bytes 1048576 | tf_op jit(solution)/shard_map/pallas_call | solution.py:45
  4.2 0.0 copy-start
  4.2 16.1 %all_to_all.50.refs_0_ = bf16[16,8,1024]{2,1,0:T(8,128)(2,1)S(1)} all-to-all(bf16[16,8,1024]{2,1,0:T(8,128)(2,1)S(1)} %get-tuple-element.44), channel_id=1, replica_groups={{8,9,10,11,12,13,14,15,16,17,18,19,20,21,22,23},{24,25,26,27,28,29,30,3..., dimensions={0} | all-to-all | bytes 524288 | tf_op jit(solution)/shard_map/all_to_all | solution.py:245
  20.3 0.0 copy-start.2
  20.3 23.1 %all_to_all.51.refs_0_ = bf16[16,8,1024]{2,1,0:T(8,128)(2,1)S(1)} all-to-all(bf16[16,8,1024]{2,1,0:T(8,128)(2,1)S(1)} %shard_map.129), channel_id=1, replica_groups={{0,1,2,3,4,5,6,7,8,9,10,11,12,13,14,15},{16,17,18,19,20,21,22,23,24,25,..., dimensions={0} | all-to-all | bytes 524288 | tf_op jit(solution)/shard_map/all_to_all | solution.py:245
  43.4 0.0 copy-done.1
  43.4 1.5 shard_map.130
  45.0 10.7 %all_to_all.52.refs_0_ = bf16[16,8,1024]{2,1,0:T(8,128)(2,1)S(1)} all-to-all(bf16[16,8,1024]{2,1,0:T(8,128)(2,1)S(1)} %get-tuple-element.48), channel_id=1, replica_groups={{8,9,10,11,12,13,14,15,16,17,18,19,20,21,22,23},{24,25,26,27,28,29,30,3..., dimensions={0} | all-to-all | bytes 524288 | tf_op jit(solution)/shard_map/all_to_all | solution.py:245
  55.7 15.5 %all_to_all.53.refs_0_ = bf16[16,8,1024]{2,1,0:T(8,128)(2,1)S(1)} all-to-all(bf16[16,8,1024]{2,1,0:T(8,128)(2,1)S(1)} %shard_map.131), channel_id=1, replica_groups={{0,1,2,3,4,5,6,7,8,9,10,11,12,13,14,15},{16,17,18,19,20,21,22,23,24,25,..., dimensions={0} | all-to-all | bytes 524288 | tf_op jit(solution)/shard_map/all_to_all | solution.py:245
  71.1 1.5 shard_map.132
  72.6 10.7 %all_to_all.54.refs_0_ = bf16[16,8,1024]{2,1,0:T(8,128)(2,1)S(1)} all-to-all(bf16[16,8,1024]{2,1,0:T(8,128)(2,1)S(1)} %get-tuple-element.50), channel_id=1, replica_groups={{8,9,10,11,12,13,14,15,16,17,18,19,20,21,22,23},{24,25,26,27,28,29,30,3..., dimensions={0} | all-to-all | bytes 524288 | tf_op jit(solution)/shard_map/all_to_all | solution.py:245
  83.4 15.5 %all_to_all.55.refs_0_ = bf16[16,8,1024]{2,1,0:T(8,128)(2,1)S(1)} all-to-all(bf16[16,8,1024]{2,1,0:T(8,128)(2,1)S(1)} %shard_map.133), channel_id=1, replica_groups={{0,1,2,3,4,5,6,7,8,9,10,11,12,13,14,15},{16,17,18,19,20,21,22,23,24,25,..., dimensions={0} | all-to-all | bytes 524288 | tf_op jit(solution)/shard_map/all_to_all | solution.py:245
  98.8 1.5 shard_map.134
  100.3 10.7 %all_to_all.56.refs_0_ = bf16[16,8,1024]{2,1,0:T(8,128)(2,1)S(1)} all-to-all(bf16[16,8,1024]{2,1,0:T(8,128)(2,1)S(1)} %get-tuple-element.52), channel_id=1, replica_groups={{8,9,10,11,12,13,14,15,16,17,18,19,20,21,22,23},{24,25,26,27,28,29,30,3..., dimensions={0} | all-to-all | bytes 524288 | tf_op jit(solution)/shard_map/all_to_all | solution.py:245
  111.1 15.5 %all_to_all.57.refs_0_ = bf16[16,8,1024]{2,1,0:T(8,128)(2,1)S(1)} all-to-all(bf16[16,8,1024]{2,1,0:T(8,128)(2,1)S(1)} %shard_map.135), channel_id=1, replica_groups={{0,1,2,3,4,5,6,7,8,9,10,11,12,13,14,15},{16,17,18,19,20,21,22,23,24,25,..., dimensions={0} | all-to-all | bytes 524288 | tf_op jit(solution)/shard_map/all_to_all | solution.py:245
  126.5 1.5 shard_map.136
  128.0 11.4 %all_to_all.58.refs_0_ = bf16[16,8,1280]{2,1,0:T(8,128)(2,1)S(1)} all-to-all(bf16[16,8,1280]{2,1,0:T(8,128)(2,1)S(1)} %get-tuple-element.58), channel_id=1, replica_groups={{0,1,2,3,4,5,6,7,8,9,10,11,12,13,14,15},{16,17,18,19,20,21,22,23,24,25,..., dimensions={0} | all-to-all | bytes 655360 | tf_op jit(solution)/shard_map/all_to_all | solution.py:245
  139.4 0.7 shard_map.137
  140.2 3.5 %all-to-all-start.9 = ((bf16[16,8,1024]{2,1,0:T(8,128)(2,1)}), bf16[16,8,1024]{2,1,0:T(8,128)(2,1)S(1)}, u32[]{:S(2)}, u32[]{:S(2)}) async-start(bf16[16,8,1024]{2,1,0:T(8,128)(2,1)} %get-tuple-element.59), calls=%async_computation.9 | async-start | bytes 524288 | tf_op jit(solution)/shard_map/all_to_all | solution.py:245
  143.6 1.7 %shard_map.139 = bf16[1024,512]{1,0:T(8,128)(2,1)} custom-call(bf16[64,1024]{1,0:T(8,128)(2,1)S(1)} %get-tuple-element.62.refs_0_, bf16[64,1024]{1,0:T(8,128)(2,1)S(1)} %get-tuple-element.63.refs_1_, bf16[64,1024]{1,0:T(8,128)(2,1)S(1)} %get-tuple-element.64.refs_2_, bf16[64,1024]{1,0:T(8,128)(2,1)S(1)} %get-tuple-element.65.refs_3_, ...), custom_call_target="tpu_custom_call" | custom-call | flops 335544320 | bytes 1048576 | tf_op jit(solution)/shard_map/pallas_call | solution.py:45
  145.4 1.7 %shard_map.140 = bf16[512,1024]{1,0:T(8,128)(2,1)} custom-call(bf16[64,512]{1,0:T(8,128)(2,1)S(1)} %get-tuple-element.72.refs_0_, bf16[64,512]{1,0:T(8,128)(2,1)S(1)} %get-tuple-element.73.refs_1_, bf16[64,512]{1,0:T(8,128)(2,1)S(1)} %get-tuple-element.74.refs_2_, bf16[64,512]{1,0:T(8,128)(2,1)S(1)} %get-tuple-element.75.refs_3_, ...), custom_call_target="tpu_custom_call" | custom-call | flops 335544320 | bytes 1048576 | tf_op jit(solution)/shard_map/pallas_call | solution.py:45
  147.1 4.3 %all-to-all-done.9.refs_0_ = bf16[16,8,1024]{2,1,0:T(8,128)(2,1)S(1)} async-done(((bf16[16,8,1024]{2,1,0:T(8,128)(2,1)}), bf16[16,8,1024]{2,1,0:T(8,128)(2,1)S(1)}, u32[]{:S(2)}, u32[]{:S(2)}) %all-to-all-start.9) | async-done | bytes 262176 | tf_op jit(solution)/shard_map/all_to_all | solution.py:245
  151.4 0.7 shard_map.138
  (6 shorter events, 0.2 us)
Async XLA Ops:
  0.6 42.8 %copy-start.1 = (bf16[1,512,1024]{2,1,0:T(8,128)(2,1)S(1)}, bf16[1,512,1024]{2,1,0:T(8,128)(2,1)}, u32[]{:S(2)}) copy-start(bf16[1,512,1024]{2,1,0:T(8,128)(2,1)} %param.16) | copy-start | bytes 3145732
  4.2 39.3 %copy-start = (bf16[1,1024,512]{2,1,0:T(8,128)(2,1)S(1)}, bf16[1,1024,512]{2,1,0:T(8,128)(2,1)}, u32[]{:S(2)}) copy-start(bf16[1,1024,512]{2,1,0:T(8,128)(2,1)} %param.15) | copy-start | bytes 3145732
  20.3 23.1 %copy-start.2 = (bf16[1,1024]{1,0:T(2,128)(2,1)S(1)}, bf16[1,1024]{1,0:T(2,128)(2,1)}, u32[]{:S(2)}) copy-start(bf16[1,1024]{1,0:T(2,128)(2,1)} %refs_2_.7) | copy-start | bytes 6148
  140.2 11.2 %all-to-all-start.9 = ((bf16[16,8,1024]{2,1,0:T(8,128)(2,1)}), bf16[16,8,1024]{2,1,0:T(8,128)(2,1)S(1)}, u32[]{:S(2)}, u32[]{:S(2)}) async-start(bf16[16,8,1024]{2,1,0:T(8,128)(2,1)} %get-tuple-element.59), calls=%async_computation.9 | async-start | bytes 524288 | tf_op jit(solution)/shard_map/all_to_all | solution.py:245

commit v5 on v4

--- a/solution.py
+++ b/solution.py
@@ -75,9 +75,8 @@
     return cdf + (0.5 * ROOT) * preact * (1.0 - tanh * tanh) * (1.0 + (3.0 * CUBE) * square)
 
 
-def flat(ref, peers, start):
-    part = ref[start : start + peers].astype(F32)
-    return part.reshape(part.shape[0] * part.shape[1], part.shape[2])
+def flat(part):
+    return part.astype(F32).reshape(part.shape[0] * part.shape[1], part.shape[2])
 
 
 def first_kernel(peers, *refs):
@@ -107,10 +106,22 @@
     planned.wait()
     fetches.append(begin(stashed.at[plan[0, 0]], slot_ref))
     others += [begin(stashed.at[plan[0, 1 + k]], target) for k, target in enumerate(later)]
-    for fetch in fetches:
-        fetch.wait()
-    inputs, grads_low = rows_ref[...].astype(F32), grads_ref[...]
-    results = both_ways(peers, inputs, grads_low.astype(F32), grads_low, slot_ref, gain_ref, weight_in, weight_out, kept)
+
+    def load_grads():
+        for fetch in fetches[:2]:
+            fetch.wait()
+        return grads_ref[...].astype(F32)
+
+    def load_inputs():
+        for fetch in fetches[2:5]:
+            fetch.wait()
+        return rows_ref[...].astype(F32)
+
+    def load_slot():
+        fetches[5].wait()
+        return slot_ref[...].astype(F32)
+
+    results = both_ways(peers, load_grads, load_inputs, load_slot, gain_ref, weight_in, weight_out, kept)
     place(peers, parts_out, *results[:2])
     kept[4][...] = results[2]
     for other in others:
@@ -120,24 +131,31 @@
 def later_kernel(peers, last, *refs):
     received, slot_ref, gain_ref, weight_in, weight_out, *gains = refs[: -5 if last else -6]
     parts_out, *kept = refs[-5 if last else -6 :]
-    inputs, grads = flat(received, peers, 0), flat(received, peers, peers)
     forward, backward, gain_sum = both_ways(
-        peers, inputs, grads, grads.astype(BF16), slot_ref, gain_ref, weight_in, weight_out, kept
+        peers,
+        lambda: flat(received[peers:]),
+        lambda: flat(received[:peers]),
+        lambda: slot_ref[...].astype(F32),
+        gain_ref,
+        weight_in,
+        weight_out,
+        kept,
     )
     if not last:
         place(peers, parts_out, forward, backward)
         kept[4][...] = gain_sum
         return
-    parts_out[:peers, :, :D] = forward
-    parts_out[peers:, :, :D] = backward
+    share = forward.shape[1]
+    parts_out[:, :share, :D] = forward
+    parts_out[:, share:, :D] = backward
     for ref in gains:
         gain_sum = gain_sum + ref[...]
     stack = jnp.concatenate([gain_sum[:, k * LANES : (k + 1) * LANES] for k in range(D // LANES)], axis=0)
     high = stack.astype(BF16)
     low = (stack - high.astype(F32)).astype(BF16)
-    for k in range(2 * peers):
-        parts_out[k, :, D : D + LANES] = high
-        parts_out[k, :, D + LANES :] = low
+    for k in range(peers):
+        parts_out[k, :share, D:] = high
+        parts_out[k, share:, D:] = low
 
 
 def place(peers, parts_out, forward, backward):
@@ -145,16 +163,18 @@
     parts_out[peers:] = forward
 
 
-def both_ways(peers, inputs, grads, grads_low, slot_ref, gain_ref, weight_in, weight_out, kept):
+def both_ways(peers, load_grads, load_inputs, load_slot, gain_ref, weight_in, weight_out, kept):
     hidden_out, scaled_out, grads_out, update_out = kept[:4]
+    grads = load_grads()
+    grads_low = grads.astype(BF16)
     grads_out[...] = grads_low
+    hidden_grad = against_rows(grads_low, weight_out[...])
+    inputs = load_inputs()
     gain = gain_ref[...].astype(F32)
     portion = 1.0 / peers
     share = inputs.shape[0] // peers
-
-    hidden_grad = against_rows(grads_low, weight_out[...])
     _, inverse, projected = normalize(inputs, gain, weight_in[...])
-    slot = slot_ref[...].astype(F32)
+    slot = load_slot()
     slot_scaled, slot_inverse, slot_projected = normalize(slot, gain, weight_in[...])
     scaled_out[...] = slot_scaled
 
@@ -189,19 +209,14 @@
 
 
 def last_sum_kernel(peers, received, spread_out, gain_out):
-    for start in (0, peers):
-        total = received[start, :, :D].astype(F32)
-        for k in range(1, peers):
-            total = total + received[start + k, :, :D].astype(F32)
-        total = total.astype(BF16)
-        for k in range(peers):
-            spread_out[start + k] = total
-    own = lax.rem(lax.axis_index("section"), 2) * peers
-    total = jnp.zeros((D // LANES, LANES), F32)
+    total = received[0].astype(F32)
+    for k in range(1, peers):
+        total = total + received[k].astype(F32)
+    piece = total[:, :D].astype(BF16)
     for k in range(peers):
-        total = total + received[own + k, :, D : D + LANES].astype(F32)
-        total = total + received[own + k, :, D + LANES :].astype(F32)
-    gain_out[...] = total
+        spread_out[k] = piece
+    share = total.shape[0] // 2
+    gain_out[...] = total[:share, D:] + total[share:, D:]
 
 
 def update_kernel(steps, *refs):
@@ -213,9 +228,10 @@
     out[...] = across_rows(left[...], right[...]).astype(BF16)
 
 
-def finish_kernel(peers, received, outputs, input_grad):
-    outputs[...] = flat(received, peers, 0).astype(BF16)
-    input_grad[...] = flat(received, peers, peers).astype(BF16)
+def finish_kernel(received, outputs, input_grad):
+    share = received.shape[1] // 2
+    outputs[...] = flat(received[:, :share]).astype(BF16)
+    input_grad[...] = flat(received[:, share:]).astype(BF16)
 
 
 def local(
@@ -244,15 +260,15 @@
     def exchange(parts, groups):
         return in_vmem(lax.all_to_all(parts, BOTH, 0, 0, axis_index_groups=groups, tiled=True))
 
-    def spread(kernel, more, *args):
-        outs = [((2 * peers, share, D), BF16, "vmem")] + more
-        return call(kernel, outs, args, 1 << 18)
+    def exchange_within(parts):
+        return in_vmem(lax.all_to_all(parts, "mp", 0, 0, tiled=True))
 
     kept = [((rows, width), BF16), ((rows, D), BF16), ((rows, D), BF16), ((rows, width), BF16), ((1, D), F32)]
     stored = [[] for _ in kept]
     for step in range(steps):
         last = step + 1 == steps
-        outs = [((2 * peers, share, D + 2 * LANES if last else D), BF16, "vmem")]
+        whole = (peers, 2 * share, D + LANES) if last else (2 * peers, share, D)
+        outs = [(whole, BF16, "vmem")]
         outs += [(shape, dtype, "vmem") for shape, dtype in kept[: 4 if last else 5]]
         if step == 0:
             args = [slot_order, stashed, arrive_rows[0], arrive_grads[0], norm_gain, *weights, feed_rows, feed_grads]
@@ -275,18 +291,15 @@
         if last:
             break
         kernel = lambda *refs: sum_kernel(peers, sections, step, *refs)
-        (parts,) = spread(kernel, [], exchange(parts, odd_pairs), *feeds)
+        args = (exchange(parts, odd_pairs), *feeds)
+        (parts,) = call(kernel, [((2 * peers, share, D), BF16, "vmem")], args, 1 << 18)
         source = exchange(parts, even_pairs)
-    received = exchange(parts, even_pairs)
-
-    parts, gain_total = spread(
-        lambda *refs: last_sum_kernel(peers, *refs),
-        [((D // LANES, LANES), F32, "any")],
-        received,
-    )
-    received = exchange(parts, even_pairs)
-    kernel = lambda *refs: finish_kernel(peers, *refs)
-    outputs, input_grad = call(kernel, [((rows, D), BF16, "any")] * 2, (received,), 1 << 18)
+
+    kernel = lambda *refs: last_sum_kernel(peers, *refs)
+    outs = [((peers, 2 * share, D), BF16, "vmem"), ((share, LANES), F32, "any")]
+    parts, gain_total = call(kernel, outs, (exchange_within(parts),), 1 << 18)
+    outs = [((rows, D), BF16, "any")] * 2
+    outputs, input_grad = call(finish_kernel, outs, (exchange_within(parts),), 1 << 18)
     totals = []
     for left, right in ((stored[0], stored[2]), (stored[1], stored[3])):
         shape = (left[0].shape[1], right[0].shape[1])

time: 153 us -> 149 us (0.974)
  blocking collectives: 129 us -> 127 us
  waiting for transfers between devices: 4.33 us -> 2.61 us
    all_to_all x9 -> x8, blocking collectives: 129 us -> 118 us  [exchange(): lax.all_to_all(parts, BOTH, 0, 0, axis_index_groups=groups, tiled=True)]
    all_to_all x0 -> x1, blocking collectives: none -> 9.65 us  [exchange_within(): return in_vmem(lax.all_to_all(parts, 'mp', 0, 0, tiled=True))]
    all_to_all x1, waiting for transfers between devices: 4.33 us -> 2.61 us  [exchange_within(): return in_vmem(lax.all_to_all(parts, 'mp', 0, 0, tiled=True))]
where the time goes in v5:
time: 149 us; the launch traced here: 148 us
  blocking collectives  127 us (85%)
  Pallas kernels  14.3 us (10%)
  starting transfers between devices  3.41 us (2%)
  waiting for transfers between devices  2.61 us (2%)
    all_to_all x8, blocking collectives, exchange(): lax.all_to_all(parts, BOTH, 0, 0, axis_index_groups=groups, tiled=True)  118 us
    pallas_call x13, Pallas kernels, call(): pl.pallas_call(kernel, out_shape=[{'vmem': pltpu.VMEM, 'hbm': pltpu.HBM,...  14.3 us
    all_to_all x1, blocking collectives, exchange_within(): return in_vmem(lax.all_to_all(parts, 'mp', 0, 0, tiled=True))  9.65 us
    all_to_all x1, starting transfers between devices, exchange_within(): return in_vmem(lax.all_to_all(parts, 'mp', 0, 0, tiled=True))  3.41 us
  transfers between devices with their start and end apart: 1, of which 1 were waited for; matrix products, arithmetic and copies ran while one was open for 0% of the time, Pallas kernels for 2%

profile of v5, /device:TPU:1, one launch (start us, length us, event | category | flops | bytes accessed | tf_op | source)
XLA Modules:
  0.0 148.3 jit_solution(11423406438378585924)
XLA Ops:
  0.6 0.0 copy-start.1
  0.6 3.2 %shard_map.128 = (bf16[16,8,1024]{2,1,0:T(8,128)(2,1)S(1)}, bf16[64,512]{1,0:T(8,128)(2,1)S(1)}, bf16[64,1024]{1,0:T(8,128)(2,1)S(1)}, bf16[64,1024]{1,0:T(8,128...) custom-call(s32[1,5]{1,0:T(1,128)} %refs_0_.1, ...), custom_call_target="tpu_custom_call" | custom-call | flops 335544320 | bytes 1048576 | tf_op jit(solution)/shard_map/pallas_call | solution.py:45
  3.9 0.0 copy-start
  3.9 16.1 %all_to_all.50.refs_0_ = bf16[16,8,1024]{2,1,0:T(8,128)(2,1)S(1)} all-to-all(bf16[16,8,1024]{2,1,0:T(8,128)(2,1)S(1)} %get-tuple-element.44), channel_id=1, replica_groups={{8,9,10,11,12,13,14,15,16,17,18,19,20,21,22,23},{24,25,26,27,28,29,30,3..., dimensions={0} | all-to-all | bytes 524288 | tf_op jit(solution)/shard_map/all_to_all | solution.py:261
  20.0 0.0 copy-start.2
  20.0 23.1 %all_to_all.51.refs_0_ = bf16[16,8,1024]{2,1,0:T(8,128)(2,1)S(1)} all-to-all(bf16[16,8,1024]{2,1,0:T(8,128)(2,1)S(1)} %shard_map.129), channel_id=1, replica_groups={{0,1,2,3,4,5,6,7,8,9,10,11,12,13,14,15},{16,17,18,19,20,21,22,23,24,25,..., dimensions={0} | all-to-all | bytes 524288 | tf_op jit(solution)/shard_map/all_to_all | solution.py:261
  43.1 0.0 copy-done
  43.2 1.5 %shard_map.130 = (bf16[16,8,1024]{2,1,0:T(8,128)(2,1)S(1)}, bf16[64,512]{1,0:T(8,128)(2,1)S(1)}, bf16[64,1024]{1,0:T(8,128)(2,1)S(1)}, bf16[64,1024]{1,0:T(8,128...) custom-call(bf16[16,8,1024]{2,1,0:T(8,128)(2,1)S(1)} %all_to_all.51.refs_0_, ...), custom_call_target="tpu_custom_call" | custom-call | flops 335544320 | bytes 1048576 | tf_op jit(solution)/shard_map/pallas_call | solution.py:45
  44.7 10.7 %all_to_all.52.refs_0_ = bf16[16,8,1024]{2,1,0:T(8,128)(2,1)S(1)} all-to-all(bf16[16,8,1024]{2,1,0:T(8,128)(2,1)S(1)} %get-tuple-element.48), channel_id=1, replica_groups={{8,9,10,11,12,13,14,15,16,17,18,19,20,21,22,23},{24,25,26,27,28,29,30,3..., dimensions={0} | all-to-all | bytes 524288 | tf_op jit(solution)/shard_map/all_to_all | solution.py:261
  55.4 15.5 %all_to_all.53.refs_0_ = bf16[16,8,1024]{2,1,0:T(8,128)(2,1)S(1)} all-to-all(bf16[16,8,1024]{2,1,0:T(8,128)(2,1)S(1)} %shard_map.131), channel_id=1, replica_groups={{0,1,2,3,4,5,6,7,8,9,10,11,12,13,14,15},{16,17,18,19,20,21,22,23,24,25,..., dimensions={0} | all-to-all | bytes 524288 | tf_op jit(solution)/shard_map/all_to_all | solution.py:261
  70.9 1.5 %shard_map.132 = (bf16[16,8,1024]{2,1,0:T(8,128)(2,1)S(1)}, bf16[64,512]{1,0:T(8,128)(2,1)S(1)}, bf16[64,1024]{1,0:T(8,128)(2,1)S(1)}, bf16[64,1024]{1,0:T(8,128...) custom-call(bf16[16,8,1024]{2,1,0:T(8,128)(2,1)S(1)} %all_to_all.53.refs_0_, ...), custom_call_target="tpu_custom_call" | custom-call | flops 335544320 | bytes 1048576 | tf_op jit(solution)/shard_map/pallas_call | solution.py:45
  72.4 10.7 %all_to_all.54.refs_0_ = bf16[16,8,1024]{2,1,0:T(8,128)(2,1)S(1)} all-to-all(bf16[16,8,1024]{2,1,0:T(8,128)(2,1)S(1)} %get-tuple-element.50), channel_id=1, replica_groups={{8,9,10,11,12,13,14,15,16,17,18,19,20,21,22,23},{24,25,26,27,28,29,30,3..., dimensions={0} | all-to-all | bytes 524288 | tf_op jit(solution)/shard_map/all_to_all | solution.py:261
  83.1 15.5 %all_to_all.55.refs_0_ = bf16[16,8,1024]{2,1,0:T(8,128)(2,1)S(1)} all-to-all(bf16[16,8,1024]{2,1,0:T(8,128)(2,1)S(1)} %shard_map.133), channel_id=1, replica_groups={{0,1,2,3,4,5,6,7,8,9,10,11,12,13,14,15},{16,17,18,19,20,21,22,23,24,25,..., dimensions={0} | all-to-all | bytes 524288 | tf_op jit(solution)/shard_map/all_to_all | solution.py:261
  98.6 1.5 %shard_map.134 = (bf16[16,8,1024]{2,1,0:T(8,128)(2,1)S(1)}, bf16[64,512]{1,0:T(8,128)(2,1)S(1)}, bf16[64,1024]{1,0:T(8,128)(2,1)S(1)}, bf16[64,1024]{1,0:T(8,128...) custom-call(bf16[16,8,1024]{2,1,0:T(8,128)(2,1)S(1)} %all_to_all.55.refs_0_, ...), custom_call_target="tpu_custom_call" | custom-call | flops 335544320 | bytes 1048576 | tf_op jit(solution)/shard_map/pallas_call | solution.py:45
  100.1 10.7 %all_to_all.56.refs_0_ = bf16[16,8,1024]{2,1,0:T(8,128)(2,1)S(1)} all-to-all(bf16[16,8,1024]{2,1,0:T(8,128)(2,1)S(1)} %get-tuple-element.52), channel_id=1, replica_groups={{8,9,10,11,12,13,14,15,16,17,18,19,20,21,22,23},{24,25,26,27,28,29,30,3..., dimensions={0} | all-to-all | bytes 524288 | tf_op jit(solution)/shard_map/all_to_all | solution.py:261
  110.8 15.4 %all_to_all.57.refs_0_ = bf16[16,8,1024]{2,1,0:T(8,128)(2,1)S(1)} all-to-all(bf16[16,8,1024]{2,1,0:T(8,128)(2,1)S(1)} %shard_map.135), channel_id=1, replica_groups={{0,1,2,3,4,5,6,7,8,9,10,11,12,13,14,15},{16,17,18,19,20,21,22,23,24,25,..., dimensions={0} | all-to-all | bytes 524288 | tf_op jit(solution)/shard_map/all_to_all | solution.py:261
  126.3 1.5 %shard_map.136 = (bf16[8,16,1152]{2,1,0:T(8,128)(2,1)S(1)}, bf16[64,512]{1,0:T(8,128)(2,1)S(1)}, bf16[64,1024]{1,0:T(8,128)(2,1)S(1)}, bf16[64,1024]{1,0:T(8,128)(2,1)S(1)}, bf16[64,512]{1,0:T(8,128)(2,1)S(1)}) custom-call(bf16[16,8,1024]{2,1,0:T(8,128)(2,1)S(1)} %all_to_all.57.refs_0_, bf16[64,1024]{1,0:T(8,128)(2,1)S(1)} %get-tuple-element.53.refs_1_, ...), custom_call_target="tpu_custom_call" | custom-call | flops 335544320 | bytes 1048576 | tf_op jit(solution)/shard_map/pallas_call | solution.py:45
  127.7 9.7 %all_to_all.58.refs_0_ = bf16[8,16,1152]{2,1,0:T(8,128)(2,1)S(1)} all-to-all(bf16[8,16,1152]{2,1,0:T(8,128)(2,1)S(1)} %get-tuple-element.58), channel_id=1, replica_groups=mesh['section'=96,'mp'=8] {'mp'}, dimensions={0} | all-to-all | bytes 589824 | tf_op jit(solution)/shard_map/all_to_all | solution.py:264
  137.4 0.7 shard_map.137
  138.1 3.4 %all-to-all-start.9 = ((bf16[8,16,1024]{2,1,0:T(8,128)(2,1)}), bf16[8,16,1024]{2,1,0:T(8,128)(2,1)S(1)}, u32[]{:S(2)}, u32[]{:S(2)}) async-start(bf16[8,16,1024]{2,1,0:T(8,128)(2,1)} %get-tuple-element.59), calls=%async_computation.9 | async-start | bytes 524288 | tf_op jit(solution)/shard_map/all_to_all | solution.py:264
  141.6 1.7 %shard_map.139 = bf16[1024,512]{1,0:T(8,128)(2,1)} custom-call(bf16[64,1024]{1,0:T(8,128)(2,1)S(1)} %get-tuple-element.62.refs_0_, bf16[64,1024]{1,0:T(8,128)(2,1)S(1)} %get-tuple-element.63.refs_1_, bf16[64,1024]{1,0:T(8,128)(2,1)S(1)} %get-tuple-element.64.refs_2_, bf16[64,1024]{1,0:T(8,128)(2,1)S(1)} %get-tuple-element.65.refs_3_, ...), custom_call_target="tpu_custom_call" | custom-call | flops 335544320 | bytes 1048576 | tf_op jit(solution)/shard_map/pallas_call | solution.py:45
  143.3 1.7 %shard_map.140 = bf16[512,1024]{1,0:T(8,128)(2,1)} custom-call(bf16[64,512]{1,0:T(8,128)(2,1)S(1)} %get-tuple-element.72.refs_0_, bf16[64,512]{1,0:T(8,128)(2,1)S(1)} %get-tuple-element.73.refs_1_, bf16[64,512]{1,0:T(8,128)(2,1)S(1)} %get-tuple-element.74.refs_2_, bf16[64,512]{1,0:T(8,128)(2,1)S(1)} %get-tuple-element.75.refs_3_, ...), custom_call_target="tpu_custom_call" | custom-call | flops 335544320 | bytes 1048576 | tf_op jit(solution)/shard_map/pallas_call | solution.py:45
  145.0 2.6 %all-to-all-done.9.received = bf16[8,16,1024]{2,1,0:T(8,128)(2,1)S(1)} async-done(((bf16[8,16,1024]{2,1,0:T(8,128)(2,1)}), bf16[8,16,1024]{2,1,0:T(8,128)(2,1)S(1)}, u32[]{:S(2)}, u32[]{:S(2)}) %all-to-all-start.9) | async-done | bytes 262176 | tf_op jit(solution)/shard_map/all_to_all | solution.py:264
  147.6 0.7 shard_map.138
  (6 shorter events, 0.2 us)
Async XLA Ops:
  0.6 42.5 %copy-start.1 = (bf16[1,512,1024]{2,1,0:T(8,128)(2,1)S(1)}, bf16[1,512,1024]{2,1,0:T(8,128)(2,1)}, u32[]{:S(2)}) copy-start(bf16[1,512,1024]{2,1,0:T(8,128)(2,1)} %param.16) | copy-start | bytes 3145732
  3.9 39.3 %copy-start = (bf16[1,1024,512]{2,1,0:T(8,128)(2,1)S(1)}, bf16[1,1024,512]{2,1,0:T(8,128)(2,1)}, u32[]{:S(2)}) copy-start(bf16[1,1024,512]{2,1,0:T(8,128)(2,1)} %param.15) | copy-start | bytes 3145732
  20.0 23.1 %copy-start.2 = (bf16[1,1024]{1,0:T(2,128)(2,1)S(1)}, bf16[1,1024]{1,0:T(2,128)(2,1)}, u32[]{:S(2)}) copy-start(bf16[1,1024]{1,0:T(2,128)(2,1)} %refs_2_.7) | copy-start | bytes 6148
  138.1 9.5 %all-to-all-start.9 = ((bf16[8,16,1024]{2,1,0:T(8,128)(2,1)}), bf16[8,16,1024]{2,1,0:T(8,128)(2,1)S(1)}, u32[]{:S(2)}, u32[]{:S(2)}) async-start(bf16[8,16,1024]{2,1,0:T(8,128)(2,1)} %get-tuple-element.59), calls=%async_computation.9 | async-start | bytes 524288 | tf_op jit(solution)/shard_map/all_to_all | solution.py:264

commit v6 on v5

--- a/solution.py
+++ b/solution.py
@@ -173,9 +173,11 @@
     gain = gain_ref[...].astype(F32)
     portion = 1.0 / peers
     share = inputs.shape[0] // peers
-    _, inverse, projected = normalize(inputs, gain, weight_in[...])
     slot = load_slot()
-    slot_scaled, slot_inverse, slot_projected = normalize(slot, gain, weight_in[...])
+    rows = inputs.shape[0]
+    scaled, inverses, products = normalize(jnp.concatenate([inputs, slot], axis=0), gain, weight_in[...])
+    inverse, projected = inverses[:rows], products[:rows]
+    slot_scaled, slot_inverse, slot_projected = scaled[rows:], inverses[rows:], products[rows:]
     scaled_out[...] = slot_scaled
 
     slot_preact = slot_inverse * slot_projected

time: 149 us -> 148 us (level)
  no operation moved by 1% of the time
where the time goes in v6:
time: 148 us; the launch traced here: 147 us
  blocking collectives  127 us (86%)
  Pallas kernels  13.5 us (9%)
  starting transfers between devices  3.41 us (2%)
  waiting for transfers between devices  2.61 us (2%)
    all_to_all x8, blocking collectives, exchange(): lax.all_to_all(parts, BOTH, 0, 0, axis_index_groups=groups, tiled=True)  118 us
    pallas_call x13, Pallas kernels, call(): pl.pallas_call(kernel, out_shape=[{'vmem': pltpu.VMEM, 'hbm': pltpu.HBM,...  13.5 us
    all_to_all x1, blocking collectives, exchange_within(): return in_vmem(lax.all_to_all(parts, 'mp', 0, 0, tiled=True))  9.66 us
    all_to_all x1, starting transfers between devices, exchange_within(): return in_vmem(lax.all_to_all(parts, 'mp', 0, 0, tiled=True))  3.41 us
  transfers between devices with their start and end apart: 1, of which 1 were waited for; matrix products, arithmetic and copies ran while one was open for 0% of the time, Pallas kernels for 2%

profile of v6, /device:TPU:1, one launch (start us, length us, event | category | flops | bytes accessed | tf_op | source)
XLA Modules:
  0.0 147.5 jit_solution(4856579860307104207)
XLA Ops:
  0.6 0.0 copy-start.1
  0.6 3.1 %shard_map.128 = (bf16[16,8,1024]{2,1,0:T(8,128)(2,1)S(1)}, bf16[64,512]{1,0:T(8,128)(2,1)S(1)}, bf16[64,1024]{1,0:T(8,128)(2,1)S(1)}, bf16[64,1024]{1,0:T(8,128...) custom-call(s32[1,5]{1,0:T(1,128)} %refs_0_.1, ...), custom_call_target="tpu_custom_call" | custom-call | flops 335544320 | bytes 1048576 | tf_op jit(solution)/shard_map/pallas_call | solution.py:45
  3.7 0.0 copy-start
  3.7 16.1 %all_to_all.50.refs_0_ = bf16[16,8,1024]{2,1,0:T(8,128)(2,1)S(1)} all-to-all(bf16[16,8,1024]{2,1,0:T(8,128)(2,1)S(1)} %get-tuple-element.44), channel_id=1, replica_groups={{8,9,10,11,12,13,14,15,16,17,18,19,20,21,22,23},{24,25,26,27,28,29,30,3..., dimensions={0} | all-to-all | bytes 524288 | tf_op jit(solution)/shard_map/all_to_all | solution.py:263
  19.8 0.0 copy-start.2
  19.8 23.1 %all_to_all.51.refs_0_ = bf16[16,8,1024]{2,1,0:T(8,128)(2,1)S(1)} all-to-all(bf16[16,8,1024]{2,1,0:T(8,128)(2,1)S(1)} %shard_map.129), channel_id=1, replica_groups={{0,1,2,3,4,5,6,7,8,9,10,11,12,13,14,15},{16,17,18,19,20,21,22,23,24,25,..., dimensions={0} | all-to-all | bytes 524288 | tf_op jit(solution)/shard_map/all_to_all | solution.py:263
  43.0 0.0 copy-done.1
  43.0 1.3 shard_map.130
  44.3 10.7 %all_to_all.52.refs_0_ = bf16[16,8,1024]{2,1,0:T(8,128)(2,1)S(1)} all-to-all(bf16[16,8,1024]{2,1,0:T(8,128)(2,1)S(1)} %get-tuple-element.48), channel_id=1, replica_groups={{8,9,10,11,12,13,14,15,16,17,18,19,20,21,22,23},{24,25,26,27,28,29,30,3..., dimensions={0} | all-to-all | bytes 524288 | tf_op jit(solution)/shard_map/all_to_all | solution.py:263
  55.1 15.5 %all_to_all.53.refs_0_ = bf16[16,8,1024]{2,1,0:T(8,128)(2,1)S(1)} all-to-all(bf16[16,8,1024]{2,1,0:T(8,128)(2,1)S(1)} %shard_map.131), channel_id=1, replica_groups={{0,1,2,3,4,5,6,7,8,9,10,11,12,13,14,15},{16,17,18,19,20,21,22,23,24,25,..., dimensions={0} | all-to-all | bytes 524288 | tf_op jit(solution)/shard_map/all_to_all | solution.py:263
  70.5 1.3 shard_map.132
  71.8 10.7 %all_to_all.54.refs_0_ = bf16[16,8,1024]{2,1,0:T(8,128)(2,1)S(1)} all-to-all(bf16[16,8,1024]{2,1,0:T(8,128)(2,1)S(1)} %get-tuple-element.50), channel_id=1, replica_groups={{8,9,10,11,12,13,14,15,16,17,18,19,20,21,22,23},{24,25,26,27,28,29,30,3..., dimensions={0} | all-to-all | bytes 524288 | tf_op jit(solution)/shard_map/all_to_all | solution.py:263
  82.6 15.5 %all_to_all.55.refs_0_ = bf16[16,8,1024]{2,1,0:T(8,128)(2,1)S(1)} all-to-all(bf16[16,8,1024]{2,1,0:T(8,128)(2,1)S(1)} %shard_map.133), channel_id=1, replica_groups={{0,1,2,3,4,5,6,7,8,9,10,11,12,13,14,15},{16,17,18,19,20,21,22,23,24,25,..., dimensions={0} | all-to-all | bytes 524288 | tf_op jit(solution)/shard_map/all_to_all | solution.py:263
  98.0 1.3 shard_map.134
  99.4 10.7 %all_to_all.56.refs_0_ = bf16[16,8,1024]{2,1,0:T(8,128)(2,1)S(1)} all-to-all(bf16[16,8,1024]{2,1,0:T(8,128)(2,1)S(1)} %get-tuple-element.52), channel_id=1, replica_groups={{8,9,10,11,12,13,14,15,16,17,18,19,20,21,22,23},{24,25,26,27,28,29,30,3..., dimensions={0} | all-to-all | bytes 524288 | tf_op jit(solution)/shard_map/all_to_all | solution.py:263
  110.1 15.5 %all_to_all.57.refs_0_ = bf16[16,8,1024]{2,1,0:T(8,128)(2,1)S(1)} all-to-all(bf16[16,8,1024]{2,1,0:T(8,128)(2,1)S(1)} %shard_map.135), channel_id=1, replica_groups={{0,1,2,3,4,5,6,7,8,9,10,11,12,13,14,15},{16,17,18,19,20,21,22,23,24,25,..., dimensions={0} | all-to-all | bytes 524288 | tf_op jit(solution)/shard_map/all_to_all | solution.py:263
  125.6 1.3 shard_map.136
  126.9 9.7 %all_to_all.58.refs_0_ = bf16[8,16,1152]{2,1,0:T(8,128)(2,1)S(1)} all-to-all(bf16[8,16,1152]{2,1,0:T(8,128)(2,1)S(1)} %get-tuple-element.58), channel_id=1, replica_groups=mesh['section'=96,'mp'=8] {'mp'}, dimensions={0} | all-to-all | bytes 589824 | tf_op jit(solution)/shard_map/all_to_all | solution.py:266
  136.6 0.7 shard_map.137
  137.3 3.4 %all-to-all-start.9 = ((bf16[8,16,1024]{2,1,0:T(8,128)(2,1)}), bf16[8,16,1024]{2,1,0:T(8,128)(2,1)S(1)}, u32[]{:S(2)}, u32[]{:S(2)}) async-start(bf16[8,16,1024]{2,1,0:T(8,128)(2,1)} %get-tuple-element.59), calls=%async_computation.9 | async-start | bytes 524288 | tf_op jit(solution)/shard_map/all_to_all | solution.py:266
  140.7 1.7 %shard_map.139 = bf16[1024,512]{1,0:T(8,128)(2,1)} custom-call(bf16[64,1024]{1,0:T(8,128)(2,1)S(1)} %get-tuple-element.62.refs_0_, bf16[64,1024]{1,0:T(8,128)(2,1)S(1)} %get-tuple-element.63.refs_1_, bf16[64,1024]{1,0:T(8,128)(2,1)S(1)} %get-tuple-element.64.refs_2_, bf16[64,1024]{1,0:T(8,128)(2,1)S(1)} %get-tuple-element.65.refs_3_, ...), custom_call_target="tpu_custom_call" | custom-call | flops 335544320 | bytes 1048576 | tf_op jit(solution)/shard_map/pallas_call | solution.py:45
  142.4 1.7 %shard_map.140 = bf16[512,1024]{1,0:T(8,128)(2,1)} custom-call(bf16[64,512]{1,0:T(8,128)(2,1)S(1)} %get-tuple-element.72.refs_0_, bf16[64,512]{1,0:T(8,128)(2,1)S(1)} %get-tuple-element.73.refs_1_, bf16[64,512]{1,0:T(8,128)(2,1)S(1)} %get-tuple-element.74.refs_2_, bf16[64,512]{1,0:T(8,128)(2,1)S(1)} %get-tuple-element.75.refs_3_, ...), custom_call_target="tpu_custom_call" | custom-call | flops 335544320 | bytes 1048576 | tf_op jit(solution)/shard_map/pallas_call | solution.py:45
  144.2 2.6 %all-to-all-done.9.received = bf16[8,16,1024]{2,1,0:T(8,128)(2,1)S(1)} async-done(((bf16[8,16,1024]{2,1,0:T(8,128)(2,1)}), bf16[8,16,1024]{2,1,0:T(8,128)(2,1)S(1)}, u32[]{:S(2)}, u32[]{:S(2)}) %all-to-all-start.9) | async-done | bytes 262176 | tf_op jit(solution)/shard_map/all_to_all | solution.py:266
  146.8 0.7 shard_map.138
  (6 shorter events, 0.2 us)
Async XLA Ops:
  0.6 42.3 %copy-start.1 = (bf16[1,512,1024]{2,1,0:T(8,128)(2,1)S(1)}, bf16[1,512,1024]{2,1,0:T(8,128)(2,1)}, u32[]{:S(2)}) copy-start(bf16[1,512,1024]{2,1,0:T(8,128)(2,1)} %param.16) | copy-start | bytes 3145732
  3.7 39.3 %copy-start = (bf16[1,1024,512]{2,1,0:T(8,128)(2,1)S(1)}, bf16[1,1024,512]{2,1,0:T(8,128)(2,1)}, u32[]{:S(2)}) copy-start(bf16[1,1024,512]{2,1,0:T(8,128)(2,1)} %param.15) | copy-start | bytes 3145732
  19.8 23.1 %copy-start.2 = (bf16[1,1024]{1,0:T(2,128)(2,1)S(1)}, bf16[1,1024]{1,0:T(2,128)(2,1)}, u32[]{:S(2)}) copy-start(bf16[1,1024]{1,0:T(2,128)(2,1)} %refs_2_.7) | copy-start | bytes 6148
  137.3 9.5 %all-to-all-start.9 = ((bf16[8,16,1024]{2,1,0:T(8,128)(2,1)}), bf16[8,16,1024]{2,1,0:T(8,128)(2,1)S(1)}, u32[]{:S(2)}, u32[]{:S(2)}) async-start(bf16[8,16,1024]{2,1,0:T(8,128)(2,1)} %get-tuple-element.59), calls=%async_computation.9 | async-start | bytes 524288 | tf_op jit(solution)/shard_map/all_to_all | solution.py:266
